TPU v7x, 32 devices: a whole 2x2x4 slice. The times are simulated.
32 devices in a mesh: seq: 8 (over z, x), tp: 4 (over y, core).
Axes of the slice: x: 2, y: 2, z: 4, core: 2. Of those that a mesh axis runs over, the one named last changes fastest.
Arguments:
- layer_in: bfloat16 [6144, 2048], P('seq', 'tp'), may hold values from -6 to 6
- attn_gain: float32 [2048], replicated, may hold values from 0.1 to 1.9
- qkv_weight: bfloat16 [3, 2048, 1024], P(None, None, 'tp'), may hold values from -0.125 to 0.125
- log_decay: float32 [8, 6144], P('tp', 'seq'), may hold values from -0.1 to 0
- write_rate: float32 [8, 6144], P('tp', 'seq'), may hold values from 0 to 0.9
- head_gain: float32 [128], replicated, may hold values from 0.1 to 1.9
- out_weight: bfloat16 [1024, 2048], P('tp'), may hold values from -0.1875 to 0.1875
- ffn_gain: float32 [2048], replicated, may hold values from 0.1 to 1.9
- gate_weight: bfloat16 [2048, 2560], P(None, 'tp'), may hold values from -0.125 to 0.125
- up_weight: bfloat16 [2048, 2560], P(None, 'tp'), may hold values from -0.125 to 0.125
- down_weight: bfloat16 [2560, 2048], P('tp'), may hold values from -0.125 to 0.125
Outputs:
- layer_out: bfloat16 [6144, 2048], P('seq', 'tp')
All inputs are finite; a program needn't handle non-finite values.
Results may differ from a plain program's by a relative error of at most 0.014.
Values may be sent and summed in bfloat16 or wider, within the bound.
No kernel may reach another device: no remote copies, remote signals or barrier semaphores. Data moves between devices by JAX's collectives and lax.ppermute only.
A program may use at most 128 MiB of HBM per device.

v0:
```python
import jax
import jax.numpy as jnp
from jax import lax
from jax.sharding import PartitionSpec as P

norm_floor = 0.1
head_floor = 0.05
highest = lax.Precision.HIGHEST


def carried_in(shard, axis, combine, identity):
    peers, here = (lax.axis_size(axis), lax.axis_index(axis))
    everything = jax.tree.map(
        lambda part, kind: lax.all_gather(part.astype(kind), axis),
        shard,
        jax.tree.map(lambda a: jnp.bfloat16 if a.dtype == jnp.float32 else a.dtype, shard),
    )
    start = jax.tree.map(
        lambda part, zero: jnp.broadcast_to(jnp.asarray(zero, part.dtype), part.shape),
        shard,
        identity,
    )

    def lap(k, before):
        reached = k < here
        new = combine(
            before, jax.tree.map(lambda part, own: part[k].astype(own.dtype), everything, shard)
        )
        return jax.tree.map(lambda a, b: jnp.where(reached, a, b), new, before)

    return lax.fori_loop(0, peers, lap, start)


def unit_rows(vectors):
    return vectors * lax.rsqrt(jnp.sum(vectors * vectors, axis=-1, keepdims=True) + 1.0)


def compose(earlier, later):
    first_map, first_shift = earlier
    second_map, second_shift = later
    joined_map = jnp.einsum("hij,hjk->hik", second_map, first_map, precision=highest)
    joined_shift = (
        jnp.einsum("hij,hjk->hik", second_map, first_shift, precision=highest) + second_shift
    )
    return (joined_map, joined_shift)


def block_terms(queries, key_rows, values, log_decay, write_rate):
    length = key_rows.shape[2]
    width = key_rows.shape[3]
    cumul = jnp.cumsum(log_decay, axis=2)
    spread = cumul[:, :, :, None] - cumul[:, :, None, :]
    row_ids = lax.broadcasted_iota(jnp.int32, (length, length), 0)
    col_ids = lax.broadcasted_iota(jnp.int32, (length, length), 1)
    inclusive = row_ids >= col_ids
    strict = row_ids > col_ids
    weight_decay = jnp.where(inclusive, jnp.exp(jnp.minimum(spread, 0.0)), 0.0)
    key_key = jnp.einsum("hcte,hcse->hcts", key_rows, key_rows, precision=highest)
    query_key = jnp.einsum("hcte,hcse->hcts", queries, key_rows, precision=highest)
    lower_part = jnp.where(strict, write_rate[:, :, :, None] * key_key * weight_decay, 0.0)
    system = lower_part + jnp.eye(length, dtype=jnp.float32)
    growth = jnp.exp(cumul)
    right_side = jnp.concatenate(
        [write_rate[:, :, :, None] * values, (write_rate * growth)[:, :, :, None] * key_rows],
        axis=3,
    )
    solved = jax.scipy.linalg.solve_triangular(system, right_side, lower=True, unit_diagonal=True)
    wy_value = solved[:, :, :, :width]
    wy_key = solved[:, :, :, width:]
    mixing = query_key * weight_decay
    keys_tail = key_rows * jnp.exp(cumul[:, :, -1:] - cumul)[:, :, :, None]
    transfer = growth[:, :, -1][:, :, None, None] * jnp.eye(width, dtype=jnp.float32) - jnp.einsum(
        "hcte,hctf->hcef", keys_tail, wy_key, precision=highest
    )
    offset = jnp.einsum("hcte,hctf->hcef", keys_tail, wy_value, precision=highest)
    local_out = jnp.einsum("hcts,hcsf->hctf", mixing, wy_value, precision=highest)
    entry_map = growth[:, :, :, None] * queries - jnp.einsum(
        "hcts,hcse->hcte", mixing, wy_key, precision=highest
    )
    return (transfer, offset, local_out, entry_map)


def advance(carried, terms):
    return (compose(carried, terms), carried)


def body(
    layer_in,
    attn_gain,
    qkv_weight,
    log_decay,
    write_rate,
    head_gain,
    out_weight,
    ffn_gain,
    gate_weight,
    up_weight,
    down_weight,
):
    length = layer_in.shape[0]
    slice_width = layer_in.shape[1]
    width = head_gain.shape[0]
    local_heads = qkv_weight.shape[2] // width
    span = min(64, length)
    pieces = length // span
    whole_rows = lax.all_gather(layer_in, "tp", axis=1, tiled=True).astype(jnp.float32)
    normed = (
        whole_rows
        * lax.rsqrt(jnp.mean(whole_rows * whole_rows, axis=1, keepdims=True) + norm_floor)
        * attn_gain
    ).astype(jnp.bfloat16)
    projected = jnp.einsum("ld,cde->cle", normed, qkv_weight, preferred_element_type=jnp.float32)
    projected = projected.reshape(3, length, local_heads, width).transpose(0, 2, 1, 3)
    projected = projected.reshape(3, local_heads, pieces, span, width)
    queries = unit_rows(projected[0])
    key_rows = unit_rows(projected[1])
    values = projected[2]
    transfer, offset, local_out, entry_map = block_terms(
        queries,
        key_rows,
        values,
        log_decay.reshape(local_heads, pieces, span),
        write_rate.reshape(local_heads, pieces, span),
    )
    start = (
        jnp.broadcast_to(jnp.eye(width, dtype=jnp.float32), (local_heads, width, width)),
        jnp.zeros((local_heads, width, width), jnp.float32),
    )
    device_terms, before = lax.scan(
        advance, start, (transfer.transpose(1, 0, 2, 3), offset.transpose(1, 0, 2, 3))
    )
    local_out = local_out + jnp.einsum("hcte,chef->hctf", entry_map, before[1], precision=highest)
    entry_map = jnp.einsum("hcte,chef->hctf", entry_map, before[0], precision=highest)
    local_out = local_out.reshape(local_heads, length, width)
    entry_map = entry_map.reshape(local_heads, length, width)
    prefix = carried_in(device_terms, "seq", compose, start)
    heads_raw = local_out + jnp.einsum("hte,hef->htf", entry_map, prefix[1], precision=highest)
    heads_out = (
        heads_raw
        * lax.rsqrt(jnp.mean(heads_raw * heads_raw, axis=-1, keepdims=True) + head_floor)
        * head_gain
    )
    heads_out = (
        heads_out.transpose(1, 0, 2).reshape(length, local_heads * width).astype(jnp.bfloat16)
    )
    attn_terms = jnp.dot(heads_out, out_weight, preferred_element_type=jnp.float32)
    attn_whole = lax.psum(attn_terms.astype(jnp.bfloat16), "tp").astype(jnp.float32)
    residual_whole = whole_rows + attn_whole
    normed_mid = (
        residual_whole
        * lax.rsqrt(jnp.mean(residual_whole * residual_whole, axis=1, keepdims=True) + norm_floor)
        * ffn_gain
    ).astype(jnp.bfloat16)
    residual = lax.dynamic_slice_in_dim(
        residual_whole, lax.axis_index("tp") * slice_width, slice_width, 1
    )
    gate_act = jnp.dot(normed_mid, gate_weight, preferred_element_type=jnp.float32)
    up_act = jnp.dot(normed_mid, up_weight, preferred_element_type=jnp.float32)
    hidden = (jax.nn.silu(gate_act) * up_act).astype(jnp.bfloat16)
    ffn_terms = jnp.dot(hidden, down_weight, preferred_element_type=jnp.float32)
    ffn_slice = lax.psum_scatter(
        ffn_terms.astype(jnp.bfloat16), "tp", scatter_dimension=1, tiled=True
    ).astype(jnp.float32)
    return (residual + ffn_slice).astype(jnp.bfloat16)


def solution(mesh):
    placed = (
        P("seq", "tp"),
        P(),
        P(None, None, "tp"),
        P("tp", "seq"),
        P("tp", "seq"),
        P(),
        P("tp", None),
        P(),
        P(None, "tp"),
        P(None, "tp"),
        P("tp", None),
    )
    return jax.shard_map(
        body, mesh=mesh, in_specs=placed, out_specs=P("seq", "tp"), check_vma=False
    )
```

profile of v0, /device:TPU:0, one launch (start us, length us, event | category | flops | bytes accessed | tf_op | source)
XLA Modules:
  0.0 470.9 jit_solution(7454724462241438603)
XLA Ops:
  12.9 27.3 %all-gather.4.cloned.1.call-done = bf16[768,2048]{1,0:T(8,128)(2,1)} async-done(((bf16[768,512]{1,0:T(8,128)(2,1)}), bf16[768,2048]{1,0:T(8,128)(2,1)}) %all-gather.4.cloned.1.call-update) | async-done | bytes 3145744 | tf_op jit(solution)/shard_map/all_gather | solution.py:106
  40.2 2.7 fusion.19
  43.0 3.1 fusion.23
  51.3 2.3 broadcast_multiply_fusion
  56.0 4.1 fusion.36
  60.0 119.3 %custom-call.4 = f32[2,12,1,64,64]{3,4,2,1,0:T(8,128)} custom-call(f32[2,12,1,64,64]{4,3,2,1,0:T(8,128)} %fusion.36), custom_call_target="InvertDiagBlocksLowerTriangular" | custom-call | tf_op jit(solution)/shard_map/jit(_solve_triangular)/vmap(vmap())/triangular_solve | solution.py:67
  179.3 2.5 multiply_multiply_fusion
  184.1 3.2 convolution_multiply_fusion.1
  192.7 4.3 convolution_bitcast_fusion
  197.0 4.4 bitcast_subtract_fusion
  202.2 38.7 %while.31 = (s32[]{:T(128)}, f32[2,128,128]{2,1,0:T(8,128)S(1)}, f32[2,128,128]{2,1,0:T(8,128)S(1)}, f32[12,2,128,128]{3,2,0,1:T(8,128)}, f32[12,2,128,128]{3,2,...) while((s32[]{:T(128)}, f32[2,128,128]{2,1,0:T(8,128)S(1)}, ...), condition=%wide.region_5.6_spmd.clone, body=%wide.region_4.5_spmd.clone.sunk | while | flops 100761600 | bytes 1967735 | solution.py:129
  241.0 4.2 fusion.63
  245.2 2.5 convolution_add_fusion.3
  250.0 33.5 %all-gather.1 = bf16[16,128,128]{2,1,0:T(8,128)(2,1)} all-gather(bf16[2,128,128]{2,1,0:T(8,128)(2,1)S(1)} %convert_element_type.77), channel_id=3, replica_groups=mesh['seq'=8,'tp'=4] {'seq'}, dimensions={0}, use_global_device_ids=true | all-gather | bytes 589824 | tf_op jit(solution)/shard_map/all_gather | solution.py:14
  283.5 33.3 %all-gather = bf16[16,128,128]{2,1,0:T(8,128)(2,1)} all-gather(bf16[2,128,128]{2,1,0:T(8,128)(2,1)S(1)} %convert_element_type.76), channel_id=2, replica_groups=mesh['seq'=8,'tp'=4] {'seq'}, dimensions={0}, use_global_device_ids=true | all-gather | bytes 589824 | tf_op jit(solution)/shard_map/all_gather | solution.py:14
  316.8 9.1 %while.32 = (s32[]{:T(128)}, f32[2,128,128]{2,1,0:T(8,128)S(1)}, s32[]{:T(128)}, bf16[8,2,128,128]{3,2,1,0:T(8,128)(2,1)}, bf16[8,2,128,128]{3,2,1,0:T(8,128)(2,1)}, /*index=5*/s32[]{:T(128)}, s32[]{:T(128)}) while((s32[]{:T(128)}, f32[2,128,128]{2,1,0:T(8,128)S(1)}, s32[]{:T(128)}, bf16[8,2,128,128]{3,2,1,0:T(8,128)(2,1)}, ...), condition=%wide.region_7.8_spmd.clone, body=%wide.region_6.7_spmd.clone.sunk | while | flops 50495492 | bytes 789095 | solution.py:31
  326.0 2.4 multiply_reduce_fusion.1
  328.5 2.7 convolution_convert_fusion.1
  331.2 69.0 %all-reduce.2.cloned.1.call-done = bf16[768,2048]{1,0:T(8,128)(2,1)} async-done(((bf16[768,2048]{1,0:T(8,128)(2,1)}), bf16[768,2048]{1,0:T(8,128)(2,1)}) %all-reduce.2.cloned.1.call-update) | async-done | bytes 3145744 | tf_op jit(solution)/shard_map/psum | solution.py:147
  400.2 6.7 %convert_add_fusion = (f32[768,2048]{1,0:T(8,128)}, f32[768]{0:T(1024)S(1)}) fusion(bf16[768,2048]{1,0:T(8,128)(2,1)} %all-gather.4.cloned.1.call-done, bf16[768,2048]{1,0:T(8,128)(2,1)} %all-reduce.2.cloned.1.call-done), kind=kLoop, calls=%fused_computation.23 | loop fusion | flops 7863552 | bytes 12585984 | tf_op jit(solution)/shard_map/add | solution.py:148
  406.9 4.3 fusion.62
  411.2 12.5 %convolution_convert_fusion = bf16[768,2048]{1,0:T(8,128)(2,1)} fusion(bf16[640,2048]{1,0:T(8,128)(2,1)} %param.25, f32[768,640]{1,0:T(8,128)} %fusion.62, bf16[2048,640]{1,0:T(8,128)(2,1)} %param.24, f32[2048]{0:T(1024)S(1)} %copy-done.19, f32[768]{0:T(1024)S(1)} %add_rsqrt_fusion.3, bf16[768,2048]{1,0:T(8,128)(2,1)} %all-gather.4.cloned.1.call-done, ...), kind=kOutput, calls=%fused_computation.31 | convolution fusion | flops 4040491008 | bytes 16657408 | tf_op jit(solution)/shard_map/dot_general | solution.py:160
  423.6 38.0 %reduce-scatter.2.cloned.1.call-done = bf16[768,512]{1,0:T(8,128)(2,1)} async-done(((bf16[768,2048]{1,0:T(8,128)(2,1)}), bf16[768,512]{1,0:T(8,128)(2,1)}) %reduce-scatter.2.cloned.1.call-update) | async-done | bytes 786448 | tf_op jit(solution)/shard_map/reduce_scatter | solution.py:161
  461.6 2.8 add_convert_fusion
  (155 shorter events, 71.8 us)
Async XLA Ops:
  6.5 36.4 %copy-start = (bf16[3,2048,256]{2,1,0:T(8,128)(2,1)S(1)}, bf16[3,2048,256]{2,1,0:T(8,128)(2,1)}, u32[]{:S(2)}) copy-start(bf16[3,2048,256]{2,1,0:T(8,128)(2,1)} %param.17) | copy-start | bytes 9437188
  6.5 36.4 %copy-start.18 = (f32[2048]{0:T(1024)S(1)}, f32[2048]{0:T(1024)}, u32[]{:S(2)}) copy-start(f32[2048]{0:T(1024)} %param.16) | copy-start | bytes 24580
  6.5 33.6 %all-gather.4.cloned.1.call-start = ((), (), s32[]{:S(2)}) async-start(), calls=%async_computation.1 | async-start | bytes 3932160 | tf_op jit(solution)/shard_map/all_gather | solution.py:106
  7.3 392.9 %all-reduce.2.cloned.1.call-start = ((), (), s32[]{:S(2)}) async-start(), calls=%async_computation.2 | async-start | bytes 6291456 | tf_op jit(solution)/shard_map/psum | solution.py:147
  8.3 37.8 %copy-start.14 = (f32[2,12,64]{2,1,0:T(8,128)}, f32[2,12,64]{2,1,0:T(8,128)S(1)}, u32[]{:S(2)}) copy-start(f32[2,12,64]{2,1,0:T(8,128)S(1)} %mul.176) | copy-start | bytes 18436
  12.2 184.8 %copy-start.13 = (f32[128,128]{1,0:T(8,128)}, f32[128,128]{1,0:T(8,128)S(1)}, u32[]{:S(2)}) copy-start(f32[128,128]{1,0:T(8,128)S(1)} %fusion.57) | copy-start | bytes 196612
  40.2 2.8 copy-start.2
  184.1 3.2 copy-start.7
  184.1 3.2 copy-start.8
  184.1 3.2 copy-start.12
  184.1 4.8 %copy-start.4 = (f32[1,2,768,128]{3,2,1,0:T(8,128)S(1)}, f32[1,2,768,128]{3,2,1,0:T(8,128)}, u32[]{:S(2)}) copy-start(f32[1,2,768,128]{3,2,1,0:T(8,128)} %copy.35) | copy-start | bytes 2359300
  188.9 3.8 copy-start.1
  190.9 6.1 %copy-start.15 = (f32[2,12]{1,0:T(2,128)S(1)}, f32[2,12]{1,0:T(2,128)}, u32[]{:S(2)}) copy-start(f32[2,12]{1,0:T(2,128)} %slice_reduce_fusion.1) | copy-start | bytes 292
  241.0 4.2 copy-start.5
  241.0 4.2 copy-start.9
  241.0 4.2 copy-start.10
  316.8 11.5 %copy-start.16 = (f32[128]{0:T(128)S(1)}, f32[128]{0:T(128)}, u32[]{:S(2)}) copy-start(f32[128]{0:T(128)} %param.20) | copy-start | bytes 1540
  326.0 2.5 copy-start.11
  331.2 75.7 %copy-start.19 = (f32[2048]{0:T(1024)S(1)}, f32[2048]{0:T(1024)}, u32[]{:S(2)}) copy-start(f32[2048]{0:T(1024)} %param.22) | copy-start | bytes 24580
  331.2 130.4 %reduce-scatter.2.cloned.1.call-start = ((), (), s32[]{:S(2)}) async-start(), calls=%async_computation.3 | async-start | bytes 3932160 | tf_op jit(solution)/shard_map/reduce_scatter | solution.py:161
  400.2 6.7 %copy-start.3 = (bf16[768,2048]{1,0:T(8,128)(2,1)S(1)}, bf16[768,2048]{1,0:T(8,128)(2,1)}, u32[]{:S(2)}) copy-start(bf16[768,2048]{1,0:T(8,128)(2,1)} %all-gather.4.cloned.1.call-done) | copy-start | bytes 9437188
  400.2 6.7 %copy-start.6 = (bf16[768,2048]{1,0:T(8,128)(2,1)S(1)}, bf16[768,2048]{1,0:T(8,128)(2,1)}, u32[]{:S(2)}) copy-start(bf16[768,2048]{1,0:T(8,128)(2,1)} %all-reduce.2.cloned.1.call-done) | copy-start | bytes 9437188
  400.2 6.7 %copy-start.17 = (bf16[2048,640]{1,0:T(8,128)(2,1)S(1)}, bf16[2048,640]{1,0:T(8,128)(2,1)}, u32[]{:S(2)}) copy-start(bf16[2048,640]{1,0:T(8,128)(2,1)} %param.23) | copy-start | bytes 7864324
Sparse Core Ops, SparseCore 0:
  8.9 31.2 all-gather.3
  331.3 68.8 all-reduce.1
  423.8 37.8 reduce-scatter.1
where the time goes:
time: 472 us; the launch traced here: 471 us
  other arithmetic  150 us (32%)
  waiting for transfers between devices  135 us (29%)
  matrix products  90.5 us (19%)
  blocking collectives  66.8 us (14%)
  local copies, waits for them, and re-layouts  13.9 us (3%)
  between operations  13.4 us (3%)
    another operation x3, other arithmetic, block_terms(): jax.scipy.linalg.solve_triangular(system, right_side, lower=True, unit_di...  120 us
    psum x1, waiting for transfers between devices, body(): lax.psum(attn_terms.astype(jnp.bfloat16), 'tp').astype(jnp.float32)  69 us
    all_gather x2, blocking collectives, carried_in(): lax.all_gather(part.astype(kind), axis)  66.8 us
    reduce_scatter x1, waiting for transfers between devices, body(): lax.psum_scatter(ffn_terms.astype(jnp.bfloat16), 'tp', scatter_dimension=...  38 us
    all_gather x1, waiting for transfers between devices, body(): lax.all_gather(layer_in, 'tp', axis=1, tiled=True).astype(jnp.float32)  27.3 us
    dot_general x20, matrix products, compose(): jnp.einsum('hij,hjk->hik', second_map, first_shift, precision=highest)  23.6 us
    dot_general x12, matrix products, compose(): jnp.einsum('hij,hjk->hik', second_map, first_map, precision=highest)  14.2 us
    dot_general x1, matrix products, body(): ffn_terms = jnp.dot(hidden, down_weight, preferred_element_type=jnp.float32)  12.5 us
  transfers between devices with their start and end apart: 3, of which 3 were waited for; matrix products, arithmetic and copies ran while one was open for 1% of the time, Pallas kernels for 0%

commit v1 on v0

v1 whole, which is shorter than its diff:
```python
import functools

import jax
import jax.numpy as jnp
from jax import lax
from jax.experimental import pallas as pl
from jax.experimental.pallas import tpu as pltpu
from jax.sharding import PartitionSpec as P

norm_floor = 0.1
head_floor = 0.05
parts_of_block = 2
radix = 3
f32 = jnp.float32
bf16 = jnp.bfloat16
vmem = pl.BlockSpec(memory_space=pltpu.VMEM)
smem = pl.BlockSpec(memory_space=pltpu.SMEM)
roomy = pltpu.CompilerParams(vmem_limit_bytes=56 * 1024 * 1024)


def mm(a, b):
    return jnp.dot(a.astype(bf16), b.astype(bf16), preferred_element_type=f32)


def mm_nt(a, b):
    return lax.dot_general(
        a.astype(bf16), b.astype(bf16), (((1,), (1,)), ((), ())), preferred_element_type=f32
    )


def mm_tn(a, b):
    return lax.dot_general(
        a.astype(bf16), b.astype(bf16), (((0,), (0,)), ((), ())), preferred_element_type=f32
    )


def halves(a):
    high = a.astype(bf16)
    return high, (a - high.astype(f32)).astype(bf16)


def mm_split(a, b):
    a_high, a_low = a
    b_high, b_low = b
    return mm(a_high, b_high) + (mm(a_high, b_low) + mm(a_low, b_high))


def swap(x, axis, bit):
    peers = lax.axis_size(axis)
    return lax.ppermute(x, axis, [(i, i ^ bit) for i in range(peers)])


def gather_pieces(x, axis):
    bit = lax.axis_size(axis) // 2
    pieces = {0: x}
    while bit:
        pieces.update({r | bit: swap(piece, axis, bit) for r, piece in pieces.items()})
        bit //= 2
    return [pieces[r] for r in range(len(pieces))]


def scatter_pieces(pieces, axis):
    peers = lax.axis_size(axis)
    bit = 1
    while bit < peers:
        keep = [r for r in pieces if not r & bit]
        moved = {r: swap(pieces[r | bit].astype(bf16), axis, bit).astype(f32) for r in keep}
        pieces = {r: pieces[r].astype(f32) + moved[r] for r in keep}
        bit *= 2
    return pieces[0]


def unit(rows):
    return rows * lax.rsqrt(jnp.sum(rows * rows, axis=1, keepdims=True) + 1.0)


def front_kernel(*refs, peers, heads, span):
    me_ref = refs[0]
    piece_refs = refs[1 : 1 + peers]
    gain_ref, weight_ref, cumul_ref, rate_ref = refs[1 + peers : 5 + peers]
    whole_ref, local_ref, entry_ref, map_ref, proj_ref = refs[5 + peers :]
    me = me_ref[0]
    length, slice_width = piece_refs[0].shape
    width = map_ref.shape[1]
    pieces = length // span
    for r in range(peers):
        at = pl.multiple_of((me ^ r) * slice_width, slice_width)
        whole_ref[:, pl.ds(at, slice_width)] = piece_refs[r][...]
    for c in range(pieces):
        rows = whole_ref[c * span : (c + 1) * span, :].astype(f32)
        normed = (
            rows
            * lax.rsqrt(jnp.mean(rows * rows, axis=1, keepdims=True) + norm_floor)
            * gain_ref[...]
        ).astype(bf16)
        for kind in range(3):
            proj_ref[kind, c * span : (c + 1) * span, :] = jnp.dot(
                normed, weight_ref[kind], preferred_element_type=f32
            )
    row_ids = lax.broadcasted_iota(jnp.int32, (span, span), 0)
    col_ids = lax.broadcasted_iota(jnp.int32, (span, span), 1)
    eye = (row_ids == col_ids).astype(f32)
    units = [(h, c) for h in range(heads) for c in range(pieces)]

    def operands(h, c):
        at = (slice(c * span, (c + 1) * span), slice(h * width, (h + 1) * width))
        cumul_row = jnp.broadcast_to(cumul_ref[h, c : c + 1, :], (span, span))
        rate = jnp.broadcast_to(rate_ref[h, c : c + 1, :], (span, span)).T
        cumul = cumul_row.T
        decay = jnp.where(
            row_ids >= col_ids, jnp.exp(jnp.minimum(cumul - cumul_row, 0.0)), 0.0
        )
        return at, cumul, cumul_row, rate, decay

    lowers = []
    inverses = []
    for h, c in units:
        at, cumul, cumul_row, rate, decay = operands(h, c)
        keys = unit(proj_ref[(1,) + at])
        proj_ref[(1,) + at] = keys
        lower = jnp.where(row_ids > col_ids, rate * mm_nt(keys, keys) * decay, 0.0)
        lowers.append(lower)
        inverses.append(eye - jnp.where(row_ids >> 1 == col_ids >> 1, lower, 0.0))
    level = 1
    while (1 << level) < span:
        joins = (row_ids >> (level + 1) == col_ids >> (level + 1)) & (
            row_ids >> level != col_ids >> level
        )
        for u in range(len(units)):
            split = halves(inverses[u])
            inner = mm_split(halves(jnp.where(joins, lowers[u], 0.0)), split)
            inverses[u] = inverses[u] - mm_split(split, halves(inner))
        level += 1
    for h in range(heads):
        carried = jnp.concatenate(
            [
                (
                    lax.broadcasted_iota(jnp.int32, (width, width), 0)
                    == lax.broadcasted_iota(jnp.int32, (width, width), 1)
                ).astype(f32),
                jnp.zeros((width, width), f32),
            ],
            axis=1,
        )
        for c in range(pieces):
            at, cumul, cumul_row, rate, decay = operands(h, c)
            keys = proj_ref[(1,) + at]
            queries = unit(proj_ref[(0,) + at])
            rate_col = rate[:, :1]
            growth = jnp.exp(cumul[:, :1])
            last = cumul_row[:1, span - 1 :]
            right_side = jnp.concatenate(
                [rate_col * growth * keys, rate_col * proj_ref[(2,) + at]], axis=1
            )
            solved = mm(inverses[h * pieces + c], right_side)
            mixed = mm(mm_nt(queries, keys) * decay, solved)
            tail = mm_tn(keys * jnp.exp(last - cumul[:, :1]), solved)
            entry = growth * queries - mixed[:, :width]
            reached = mm(entry, carried)
            rows_at = slice(c * span, (c + 1) * span)
            entry_ref[h, rows_at, :] = reached[:, :width].astype(bf16)
            local_ref[h, rows_at, :] = reached[:, width:] + mixed[:, width:]
            change = mm(tail[:, :width], carried)
            carried = jnp.exp(last) * carried - change
            carried = jnp.concatenate(
                [carried[:, :width], carried[:, width:] + tail[:, width:]], axis=1
            )
        map_ref[h] = carried.astype(bf16)


def joined(maps, h, width):
    acc = maps[-1][h].astype(f32)
    for one in reversed(maps[:-1]):
        acc = mm(one[h, :, :width], acc)
        shift = one[h, :, width:].astype(f32)
        if acc.shape[1] == width:
            acc = acc + shift
        else:
            acc = jnp.concatenate([acc[:, :width], acc[:, width:] + shift], axis=1)
    return acc


def join_kernel(*refs):
    out_ref = refs[-1]
    width = out_ref.shape[1]
    for h in range(out_ref.shape[0]):
        out_ref[h] = joined(refs[:-1], h, width).astype(bf16)


def heads_kernel(*refs, count):
    map_refs = refs[:count]
    local_ref, entry_ref, gain_ref = refs[count : count + 3]
    out_refs = refs[count + 3 :]
    heads, length, width = local_ref.shape
    rows = length // len(out_refs)
    for h in range(heads):
        state = joined(map_refs, h, width)
        if state.shape[1] != width:
            state = state[:, width:]
        for part, out_ref in enumerate(out_refs):
            at = slice(part * rows, (part + 1) * rows)
            raw = local_ref[h, at, :] + mm(entry_ref[h, at, :], state)
            out_ref[:, h * width : (h + 1) * width] = (
                raw
                * lax.rsqrt(jnp.mean(raw * raw, axis=1, keepdims=True) + head_floor)
                * gain_ref[...]
            ).astype(bf16)


def back_kernel(*refs, peers):
    me_ref = refs[0]
    head_refs = refs[1 : 1 + peers]
    out_weight_refs = refs[1 + peers : 1 + 2 * peers]
    whole_ref, gain_ref, gate_ref, up_ref, down_ref = refs[1 + 2 * peers : 6 + 2 * peers]
    own_ref = refs[6 + 2 * peers]
    term_refs = refs[7 + 2 * peers : 7 + 3 * peers]
    residual_ref = refs[-1]
    me = me_ref[0]
    slice_width = own_ref.shape[1]
    attn = jnp.dot(head_refs[0][...], out_weight_refs[0][...], preferred_element_type=f32)
    for r in range(1, peers):
        attn = attn + jnp.dot(
            head_refs[r][...], out_weight_refs[r][...], preferred_element_type=f32
        )
    residual = whole_ref[...].astype(f32) + attn
    residual_ref[...] = residual
    normed = (
        residual
        * lax.rsqrt(jnp.mean(residual * residual, axis=1, keepdims=True) + norm_floor)
        * gain_ref[...]
    ).astype(bf16)
    gate = jnp.dot(normed, gate_ref[...], preferred_element_type=f32)
    up = jnp.dot(normed, up_ref[...], preferred_element_type=f32)
    hidden = (jax.nn.silu(gate) * up).astype(bf16)
    for r in reversed(range(peers)):
        at = pl.multiple_of((me ^ r) * slice_width, slice_width)
        term_refs[r][...] = jnp.dot(
            hidden, down_ref[:, pl.ds(at, slice_width)], preferred_element_type=f32
        ).astype(bf16)
    at = pl.multiple_of(me * slice_width, slice_width)
    own_ref[...] = residual_ref[:, pl.ds(at, slice_width)]


def call(kernel, outs, args, scratch=(), first_smem=True):
    return pl.pallas_call(
        kernel,
        out_shape=[jax.ShapeDtypeStruct(s, d) for s, d in outs],
        in_specs=[smem if first_smem and i == 0 else vmem for i in range(len(args))],
        out_specs=[vmem] * len(outs),
        scratch_shapes=list(scratch),
        compiler_params=roomy,
    )(*args)


def shifted(x, axis, by):
    peers = lax.axis_size(axis)
    return lax.ppermute(x, axis, [(i, i + by) for i in range(peers - by)])


def earlier_maps(maps, axis):
    peers = lax.axis_size(axis)
    width = maps.shape[1]
    window = 1
    while window * radix < peers - 1:
        terms = [maps] + [shifted(maps, axis, window * k) for k in range(1, radix)]
        maps = call(join_kernel, [(maps.shape, bf16)], terms, first_smem=False)[0]
        window *= radix
    offsets = list(range(1, peers, window))
    moved = [shifted(maps, axis, by) for by in offsets[:-1]]
    return moved + [shifted(maps[:, :, width:], axis, by) for by in offsets[-1:]]


def body(
    layer_in,
    attn_gain,
    qkv_weight,
    log_decay,
    write_rate,
    head_gain,
    out_weight,
    ffn_gain,
    gate_weight,
    up_weight,
    down_weight,
):
    length, slice_width = layer_in.shape
    width = head_gain.shape[0]
    local_heads = qkv_weight.shape[2] // width
    model = attn_gain.shape[0]
    peers = lax.axis_size("tp")
    me = lax.axis_index("tp").astype(jnp.int32).reshape(1)
    span = min(128, length)
    count = length // span
    pieces = gather_pieces(layer_in, "tp")
    cumul = jnp.cumsum(log_decay.reshape(local_heads, count, span), axis=2)
    held = lax.optimization_barrier((out_weight, pieces[peers // 2]))
    weight_pieces = gather_pieces(held[0], "tp")
    whole, local, entry, maps = call(
        functools.partial(front_kernel, peers=peers, heads=local_heads, span=span),
        [
            ((length, model), bf16),
            ((local_heads, length, width), f32),
            ((local_heads, length, width), bf16),
            ((local_heads, width, 2 * width), bf16),
        ],
        [
            me,
            *pieces,
            attn_gain.reshape(1, model),
            qkv_weight,
            cumul,
            write_rate.reshape(local_heads, count, span),
        ],
        scratch=[pltpu.VMEM((3, length, local_heads * width), f32)],
    )
    before = earlier_maps(maps, "seq")
    rows = length // parts_of_block
    heads_out = call(
        functools.partial(heads_kernel, count=len(before)),
        [((rows, local_heads * width), bf16)] * parts_of_block,
        [*before, local, entry, head_gain.reshape(1, width)],
        first_smem=False,
    )
    results = []
    gathered = [gather_pieces(part, "tp") for part in heads_out]
    for part in range(parts_of_block):
        own, *terms = call(
            functools.partial(back_kernel, peers=peers),
            [((rows, slice_width), f32)] + [((rows, slice_width), bf16)] * peers,
            [
                me,
                *gathered[part],
                *weight_pieces,
                lax.slice_in_dim(whole, part * rows, (part + 1) * rows),
                ffn_gain.reshape(1, model),
                gate_weight,
                up_weight,
                down_weight,
            ],
            scratch=[pltpu.VMEM((rows, model), f32)],
        )
        shared = scatter_pieces(dict(enumerate(terms)), "tp")
        results.append((own + shared).astype(bf16))
    return jnp.concatenate(results, axis=0)


def solution(mesh):
    placed = (
        P("seq", "tp"),
        P(),
        P(None, None, "tp"),
        P("tp", "seq"),
        P("tp", "seq"),
        P(),
        P("tp", None),
        P(),
        P(None, "tp"),
        P(None, "tp"),
        P("tp", None),
    )
    return jax.shard_map(
        body, mesh=mesh, in_specs=placed, out_specs=P("seq", "tp"), check_vma=False
    )
```

time: 472 us -> 158 us (0.33)
  other arithmetic: 150 us -> 3.79 us
  matrix products: 90.5 us -> 0 us
  waiting for transfers between devices: 135 us -> 67.3 us
  blocking collectives: 66.8 us -> 0 us
  Pallas kernels: 0 us -> 44.8 us
  starting transfers between devices: 0.08 us -> 29.6 us
  between operations: 13.4 us -> 0.17 us
    another operation x6 -> x1, other arithmetic: 120 us -> 1.16 us  [body(): cumul = jnp.cumsum(log_decay.reshape(local_heads, count, span), axis=2)]
    dot_general x45 -> x0, matrix products: 88.9 us -> none  [the longest x20 23.6 us: compose(): jnp.einsum('hij,hjk->hik', second_map, first_shift, precision=highest)]
    psum x1 -> x0, waiting for transfers between devices: 69 us -> none  [body(): lax.psum(attn_terms.astype(jnp.bfloat16), 'tp').astype(jnp.float32)]
    ppermute x0 -> x23, waiting for transfers between devices: none -> 67.3 us  [the longest x18 62.1 us: swap(): return lax.ppermute(x, axis, [(i, i ^ bit) for i in range(peers)])]
    all_gather x2 -> x0, blocking collectives: 66.8 us -> none  [carried_in(): lax.all_gather(part.astype(kind), axis)]
    pallas_call x0 -> x5, Pallas kernels: none -> 44.8 us  [call(): pl.pallas_call(kernel, out_shape=[jax.ShapeDtypeStruct(s, d) for s, d in...]
    reduce_scatter x1 -> x0, waiting for transfers between devices: 38 us -> none  [body(): lax.psum_scatter(ffn_terms.astype(jnp.bfloat16), 'tp', scatter_dimension=...]
    ppermute x0 -> x23, starting transfers between devices: none -> 29.6 us  [the longest x5 17 us: shifted(): return lax.ppermute(x, axis, [(i, i + by) for i in range(peers - by)])]
  transfers between devices with their start and end apart: 3 -> 23, of which waited for: 3 -> 10; matrix products, arithmetic and copies ran while one was open for 1% -> 6% of each run, Pallas kernels for 0% -> 29%
where the time goes in v1:
time: 158 us; the launch traced here: 156 us
  waiting for transfers between devices  67.3 us (43%)
  Pallas kernels  44.8 us (28%)
  starting transfers between devices  29.6 us (19%)
  local copies, waits for them, and re-layouts  10.4 us (7%)
  other arithmetic  3.79 us (2%)
    ppermute x18, waiting for transfers between devices, swap(): return lax.ppermute(x, axis, [(i, i ^ bit) for i in range(peers)])  62.1 us
    pallas_call x5, Pallas kernels, call(): pl.pallas_call(kernel, out_shape=[jax.ShapeDtypeStruct(s, d) for s, d in...  44.8 us
    ppermute x5, starting transfers between devices, shifted(): return lax.ppermute(x, axis, [(i, i + by) for i in range(peers - by)])  17 us
    ppermute x18, starting transfers between devices, swap(): return lax.ppermute(x, axis, [(i, i ^ bit) for i in range(peers)])  12.6 us
    ppermute x5, waiting for transfers between devices, shifted(): return lax.ppermute(x, axis, [(i, i + by) for i in range(peers - by)])  5.19 us
    slice x1, local copies, waits for them, and re-layouts, body(): lax.slice_in_dim(whole, part * rows, (part + 1) * rows)  4.04 us
    unnamed x42, local copies, waits for them, and re-layouts  3.48 us
  transfers between devices with their start and end apart: 23, of which 10 were waited for; matrix products, arithmetic and copies ran while one was open for 6% of the time, Pallas kernels for 29%

profile of v1, /device:TPU:0, one launch (start us, length us, event | category | flops | bytes accessed | tf_op | source)
XLA Modules:
  0.0 156.1 jit_solution(64523047298892874)
XLA Ops:
  0.0 3.0 %collective-permute-start.1 = (bf16[768,512]{1,0:T(8,128)(2,1)}, bf16[768,512]{1,0:T(8,128)(2,1)}, u32[]{:S(2)}, u32[]{:S(2)}) collective-permute-start(bf16[768,512]{1,0:T(8,128)(2,1)} %refs_1_.1), channel_id=1, source_target_pairs={{0,2},{1,3},{2,0},{3,1},{4,6},{5,7},{6,4},{7,5},{8,10},{9,11},{10,... | collective-permute-start | bytes 2359304 | tf_op jit(solution)/shard_map/ppermute | solution.py:50
  3.0 17.9 %collective-permute-done.1.refs_3_ = bf16[768,512]{1,0:T(8,128)(2,1)} collective-permute-done((bf16[768,512]{1,0:T(8,128)(2,1)}, bf16[768,512]{1,0:T(8,128)(2,1)}, u32[]{:S(2)}, u32[]{:S(2)}) %collective-permute-start.1) | collective-permute-done | bytes 786464 | tf_op jit(solution)/shard_map/ppermute | solution.py:50
  20.9 1.7 %collective-permute-start.12 = (bf16[256,2048]{1,0:T(8,128)(2,1)}, bf16[256,2048]{1,0:T(8,128)(2,1)S(1)}, u32[]{:S(2)}, u32[]{:S(2)}) collective-permute-start(bf16[256,2048]{1,0:T(8,128)(2,1)} %refs_5_.1), channel_id=1, source_target_pairs={{0,2},{1,3},{2,0},{3,1},{4,6},{5,7},{6,4},{7,5},{8,10},{9,11},{10,... | collective-permute-start | bytes 3145736 | tf_op jit(solution)/shard_map/ppermute | solution.py:50
  23.1 22.3 %collective-permute-done.12.refs_7_ = bf16[256,2048]{1,0:T(8,128)(2,1)S(1)} collective-permute-done((bf16[256,2048]{1,0:T(8,128)(2,1)}, bf16[256,2048]{1,0:T(8,128)(2,1)S(1)}, u32[]{:S(2)}, u32[]{:S(2)}) %collective-permute-start.12) | collective-permute-done | bytes 1048608 | tf_op jit(solution)/shard_map/ppermute | solution.py:50
  46.1 1.3 reshape.22.refs_8_
  48.5 15.7 %shard_map.109 = (bf16[768,2048]{1,0:T(8,128)(2,1)}, f32[2,768,128]{2,1,0:T(8,128)}, bf16[2,768,128]{2,1,0:T(8,128)(2,1)}, bf16[2,128,256]{2,1,0:T(8,128)(2,1)}) custom-call(s32[1]{0:T(128)} %bitcast.refs_0_, bf16[768,512]{1,0:T(8,128)(2,1)} %refs_1_.1, bf16[768,512]{1,0:T(8,128)(2,1)} %collective-permute-done.refs_2_, ...), custom_call_target="tpu_custom_call" | custom-call | tf_op jit(solution)/shard_map/pallas_call | solution.py:245
  64.2 3.3 %collective-permute-start.3 = (bf16[2,128,256]{2,1,0:T(8,128)(2,1)}, bf16[2,128,256]{2,1,0:T(8,128)(2,1)S(1)}, u32[]{:S(2)}, u32[]{:S(2)}) collective-permute-start(bf16[2,128,256]{2,1,0:T(8,128)(2,1)} %get-tuple-element.22.refs_0_), channel_id=1, source_target_pairs={{0,4},{4,8},{8,12},{12,16},{16,20},{20,24},{24,28},{1,5},{5,9},{9,... | collective-permute-start | bytes 393224 | tf_op jit(solution)/shard_map/ppermute | solution.py:257
  67.5 3.5 %collective-permute-start.4 = (bf16[2,128,256]{2,1,0:T(8,128)(2,1)}, bf16[2,128,256]{2,1,0:T(8,128)(2,1)S(1)}, u32[]{:S(2)}, u32[]{:S(2)}) collective-permute-start(bf16[2,128,256]{2,1,0:T(8,128)(2,1)} %get-tuple-element.22.refs_0_), channel_id=1, source_target_pairs={{0,8},{4,12},{8,16},{12,20},{16,24},{20,28},{1,9},{5,13},{9,17},{1... | collective-permute-start | bytes 393224 | tf_op jit(solution)/shard_map/ppermute | solution.py:257
  71.3 3.2 %collective-permute-done.4.refs_2_ = bf16[2,128,256]{2,1,0:T(8,128)(2,1)S(1)} collective-permute-done((bf16[2,128,256]{2,1,0:T(8,128)(2,1)}, bf16[2,128,256]{2,1,0:T(8,128)(2,1)S(1)}, u32[]{:S(2)}, u32[]{:S(2)}) %collective-permute-start.4) | collective-permute-done | bytes 131104 | tf_op jit(solution)/shard_map/ppermute | solution.py:257
  75.1 2.0 %shard_map.110 = bf16[2,128,256]{2,1,0:T(8,128)(2,1)} custom-call(bf16[2,128,256]{2,1,0:T(8,128)(2,1)} %get-tuple-element.22.refs_0_, bf16[2,128,256]{2,1,0:T(8,128)(2,1)} %copy-done.15, bf16[2,128,256]{2,1,0:T(8,128)(2,1)} %copy-done.16), custom_call_target="tpu_custom_call" | custom-call | tf_op jit(solution)/shard_map/pallas_call | solution.py:245
  77.2 3.5 %collective-permute-start.5 = (bf16[2,128,256]{2,1,0:T(8,128)(2,1)}, bf16[2,128,256]{2,1,0:T(8,128)(2,1)S(1)}, u32[]{:S(2)}, u32[]{:S(2)}) collective-permute-start(bf16[2,128,256]{2,1,0:T(8,128)(2,1)} %shard_map.110), channel_id=1, source_target_pairs={{0,4},{4,8},{8,12},{12,16},{16,20},{20,24},{24,28},{1,5},{5,9},{9,... | collective-permute-start | bytes 393224 | tf_op jit(solution)/shard_map/ppermute | solution.py:257
  80.6 5.3 %collective-permute-start.6 = (bf16[2,128,256]{2,1,0:T(8,128)(2,1)}, bf16[2,128,256]{2,1,0:T(8,128)(2,1)S(1)}, u32[]{:S(2)}, u32[]{:S(2)}) collective-permute-start(bf16[2,128,256]{2,1,0:T(8,128)(2,1)} %shard_map.110), channel_id=1, source_target_pairs={{0,16},{4,20},{8,24},{12,28},{1,17},{5,21},{9,25},{13,29},{2,18},{... | collective-permute-start | bytes 393224 | tf_op jit(solution)/shard_map/ppermute | solution.py:257
  86.8 1.5 collective-permute-start.7
  88.2 1.8 %collective-permute-done.7.refs_2_ = bf16[2,128,128]{2,1,0:T(8,128)(2,1)S(1)} collective-permute-done((bf16[2,128,128]{2,1,0:T(8,128)(2,1)S(1)}, bf16[2,128,128]{2,1,0:T(8,128)(2,1)S(1)}, u32[]{:S(2)}, u32[]{:S(2)}) %collective-permute-start.7) | collective-permute-done | bytes 65568 | tf_op jit(solution)/shard_map/ppermute | solution.py:257
  90.7 3.1 %shard_map.111 = (bf16[384,256]{1,0:T(8,128)(2,1)}, bf16[384,256]{1,0:T(8,128)(2,1)}) custom-call(bf16[2,128,256]{2,1,0:T(8,128)(2,1)} %copy-done.17, bf16[2,128,256]{2,1,0:T(8,128)(2,1)} %copy-done.18, bf16[2,128,128]{2,1,0:T(8,128)(2,1)} %copy-done.19, f32[2,768,128]{2,1,0:T(8,128)} %get-tuple-element.23.refs_3_, ...), custom_call_target="tpu_custom_call" | custom-call | tf_op jit(solution)/shard_map/pallas_call | solution.py:245
  93.8 1.5 collective-permute-start.9
  95.8 5.1 %collective-permute-done.9.refs_3_ = bf16[384,256]{1,0:T(8,128)(2,1)S(1)} collective-permute-done((bf16[384,256]{1,0:T(8,128)(2,1)}, bf16[384,256]{1,0:T(8,128)(2,1)S(1)}, u32[]{:S(2)}, u32[]{:S(2)}) %collective-permute-start.9) | collective-permute-done | bytes 196640 | tf_op jit(solution)/shard_map/ppermute | solution.py:50
  100.9 4.0 %fusion = (bf16[384,2048]{1,0:T(8,128)(2,1)}, bf16[384,2048]{1,0:T(8,128)(2,1)}) fusion(bf16[768,2048]{1,0:T(8,128)(2,1)} %get-tuple-element.27), kind=kLoop, calls=%fused_computation.5 | loop fusion | bytes 6291456 | tf_op jit(solution)/shard_map/slice | solution.py:334
  106.4 12.1 %shard_map.112 = (f32[384,512]{1,0:T(8,128)}, bf16[384,512]{1,0:T(8,128)(2,1)}, bf16[384,512]{1,0:T(8,128)(2,1)}, bf16[384,512]{1,0:T(8,128)(2,1)}, bf16[384,512]{1,0:T(8,128)(2,1)}) custom-call(s32[1]{0:T(128)} %bitcast.refs_0_, bf16[384,256]{1,0:T(8,128)(2,1)} %get-tuple-element.25.refs_1_, bf16[384,256]{1,0:T(8,128)(2,1)} %copy-done.11, ...), custom_call_target="tpu_custom_call" | custom-call | tf_op jit(solution)/shard_map/pallas_call | solution.py:245
  119.4 1.3 collective-permute-done.17.refs_2_
  121.7 12.0 %shard_map.113 = (f32[384,512]{1,0:T(8,128)}, bf16[384,512]{1,0:T(8,128)(2,1)}, bf16[384,512]{1,0:T(8,128)(2,1)}, bf16[384,512]{1,0:T(8,128)(2,1)}, bf16[384,512]{1,0:T(8,128)(2,1)}) custom-call(s32[1]{0:T(128)} %bitcast.refs_0_, bf16[384,256]{1,0:T(8,128)(2,1)} %get-tuple-element.33.refs_1_, bf16[384,256]{1,0:T(8,128)(2,1)} %copy-done.12, ...), custom_call_target="tpu_custom_call" | custom-call | tf_op jit(solution)/shard_map/pallas_call | solution.py:245
  134.4 2.4 %collective-permute-start.16 = (bf16[384,512]{1,0:T(8,128)(2,1)S(1)}, bf16[384,512]{1,0:T(8,128)(2,1)S(1)}, u32[]{:S(2)}, u32[]{:S(2)}) collective-permute-start(bf16[384,512]{1,0:T(8,128)(2,1)S(1)} %add_convert_fusion.3), channel_id=1, source_target_pairs={{0,2},{1,3},{2,0},{3,1},{4,6},{5,7},{6,4},{7,5},{8,10},{9,11},{10,... | collective-permute-start | bytes 1179656 | tf_op jit(solution)/shard_map/ppermute | solution.py:50
  139.4 7.4 %collective-permute-done.16 = bf16[384,512]{1,0:T(8,128)(2,1)S(1)} collective-permute-done((bf16[384,512]{1,0:T(8,128)(2,1)S(1)}, bf16[384,512]{1,0:T(8,128)(2,1)S(1)}, u32[]{:S(2)}, u32[]{:S(2)}) %collective-permute-start.16) | collective-permute-done | bytes 393248 | tf_op jit(solution)/shard_map/ppermute | solution.py:50
  147.0 7.9 %collective-permute-done.22 = bf16[384,512]{1,0:T(8,128)(2,1)S(1)} collective-permute-done((bf16[384,512]{1,0:T(8,128)(2,1)S(1)}, bf16[384,512]{1,0:T(8,128)(2,1)S(1)}, u32[]{:S(2)}, u32[]{:S(2)}) %collective-permute-start.22) | collective-permute-done | bytes 393248 | tf_op jit(solution)/shard_map/ppermute | solution.py:50
  (79 shorter events, 13.2 us)
Async XLA Ops:
  0.0 20.8 %collective-permute-start.1 = (bf16[768,512]{1,0:T(8,128)(2,1)}, bf16[768,512]{1,0:T(8,128)(2,1)}, u32[]{:S(2)}, u32[]{:S(2)}) collective-permute-start(bf16[768,512]{1,0:T(8,128)(2,1)} %refs_1_.1), channel_id=1, source_target_pairs={{0,2},{1,3},{2,0},{3,1},{4,6},{5,7},{6,4},{7,5},{8,10},{9,11},{10,... | collective-permute-start | bytes 2359304 | tf_op jit(solution)/shard_map/ppermute | solution.py:50
  20.9 24.5 %collective-permute-start.12 = (bf16[256,2048]{1,0:T(8,128)(2,1)}, bf16[256,2048]{1,0:T(8,128)(2,1)S(1)}, u32[]{:S(2)}, u32[]{:S(2)}) collective-permute-start(bf16[256,2048]{1,0:T(8,128)(2,1)} %refs_5_.1), channel_id=1, source_target_pairs={{0,2},{1,3},{2,0},{3,1},{4,6},{5,7},{6,4},{7,5},{8,10},{9,11},{10,... | collective-permute-start | bytes 3145736 | tf_op jit(solution)/shard_map/ppermute | solution.py:50
  22.6 26.0 %collective-permute-start = (bf16[768,512]{1,0:T(8,128)(2,1)}, bf16[768,512]{1,0:T(8,128)(2,1)}, u32[]{:S(2)}, u32[]{:S(2)}) collective-permute-start(bf16[768,512]{1,0:T(8,128)(2,1)} %refs_1_.1), channel_id=1, source_target_pairs={{0,1},{1,0},{2,3},{3,2},{4,5},{5,4},{6,7},{7,6},{8,9},{9,8},{10,11... | collective-permute-start | bytes 2359304 | tf_op jit(solution)/shard_map/ppermute | solution.py:50
  22.6 26.0 %collective-permute-start.2 = (bf16[768,512]{1,0:T(8,128)(2,1)}, bf16[768,512]{1,0:T(8,128)(2,1)}, u32[]{:S(2)}, u32[]{:S(2)}) collective-permute-start(bf16[768,512]{1,0:T(8,128)(2,1)} %collective-permute-done.1.refs_3_), channel_id=1, source_target_pairs={{0,1},{1,0},{2,3},{3,2},{4,5},{5,4},{6,7},{7,6},{8,9},{9,8},{10,11... | collective-permute-start | bytes 2359304 | tf_op jit(solution)/shard_map/ppermute | solution.py:50
  23.1 81.8 %collective-permute-start.11 = (bf16[256,2048]{1,0:T(8,128)(2,1)}, bf16[256,2048]{1,0:T(8,128)(2,1)S(1)}, u32[]{:S(2)}, u32[]{:S(2)}) collective-permute-start(bf16[256,2048]{1,0:T(8,128)(2,1)} %refs_5_.1), channel_id=1, source_target_pairs={{0,1},{1,0},{2,3},{3,2},{4,5},{5,4},{6,7},{7,6},{8,9},{9,8},{10,11... | collective-permute-start | bytes 3145736 | tf_op jit(solution)/shard_map/ppermute | solution.py:50
  45.4 18.8 %copy-start = (bf16[256,2048]{1,0:T(8,128)(2,1)}, bf16[256,2048]{1,0:T(8,128)(2,1)S(1)}, u32[]{:S(2)}) copy-start(bf16[256,2048]{1,0:T(8,128)(2,1)S(1)} %collective-permute-done.12.refs_7_) | copy-start | bytes 3145732
  45.4 59.6 %collective-permute-start.13 = (bf16[256,2048]{1,0:T(8,128)(2,1)S(1)}, bf16[256,2048]{1,0:T(8,128)(2,1)S(1)}, u32[]{:S(2)}, u32[]{:S(2)}) collective-permute-start(bf16[256,2048]{1,0:T(8,128)(2,1)S(1)} %collective-permute-done.12.refs_7_), channel_id=1, source_target_pairs={{0,1},{1,0},{2,3},{3,2},{4,5},{5,4},{6,7},{7,6},{8,9},{9,8},{10,11... | collective-permute-start | bytes 3145736 | tf_op jit(solution)/shard_map/ppermute | solution.py:50
  64.2 7.1 %collective-permute-start.3 = (bf16[2,128,256]{2,1,0:T(8,128)(2,1)}, bf16[2,128,256]{2,1,0:T(8,128)(2,1)S(1)}, u32[]{:S(2)}, u32[]{:S(2)}) collective-permute-start(bf16[2,128,256]{2,1,0:T(8,128)(2,1)} %get-tuple-element.22.refs_0_), channel_id=1, source_target_pairs={{0,4},{4,8},{8,12},{12,16},{16,20},{20,24},{24,28},{1,5},{5,9},{9,... | collective-permute-start | bytes 393224 | tf_op jit(solution)/shard_map/ppermute | solution.py:257
  67.5 6.9 %collective-permute-start.4 = (bf16[2,128,256]{2,1,0:T(8,128)(2,1)}, bf16[2,128,256]{2,1,0:T(8,128)(2,1)S(1)}, u32[]{:S(2)}, u32[]{:S(2)}) collective-permute-start(bf16[2,128,256]{2,1,0:T(8,128)(2,1)} %get-tuple-element.22.refs_0_), channel_id=1, source_target_pairs={{0,8},{4,12},{8,16},{12,20},{16,24},{20,28},{1,9},{5,13},{9,17},{1... | collective-permute-start | bytes 393224 | tf_op jit(solution)/shard_map/ppermute | solution.py:257
  77.2 12.8 %collective-permute-start.5 = (bf16[2,128,256]{2,1,0:T(8,128)(2,1)}, bf16[2,128,256]{2,1,0:T(8,128)(2,1)S(1)}, u32[]{:S(2)}, u32[]{:S(2)}) collective-permute-start(bf16[2,128,256]{2,1,0:T(8,128)(2,1)} %shard_map.110), channel_id=1, source_target_pairs={{0,4},{4,8},{8,12},{12,16},{16,20},{20,24},{24,28},{1,5},{5,9},{9,... | collective-permute-start | bytes 393224 | tf_op jit(solution)/shard_map/ppermute | solution.py:257
  80.6 9.4 %collective-permute-start.6 = (bf16[2,128,256]{2,1,0:T(8,128)(2,1)}, bf16[2,128,256]{2,1,0:T(8,128)(2,1)S(1)}, u32[]{:S(2)}, u32[]{:S(2)}) collective-permute-start(bf16[2,128,256]{2,1,0:T(8,128)(2,1)} %shard_map.110), channel_id=1, source_target_pairs={{0,16},{4,20},{8,24},{12,28},{1,17},{5,21},{9,25},{13,29},{2,18},{... | collective-permute-start | bytes 393224 | tf_op jit(solution)/shard_map/ppermute | solution.py:257
  86.8 3.2 %collective-permute-start.7 = (bf16[2,128,128]{2,1,0:T(8,128)(2,1)S(1)}, bf16[2,128,128]{2,1,0:T(8,128)(2,1)S(1)}, u32[]{:S(2)}, u32[]{:S(2)}) collective-permute-start(bf16[2,128,128]{2,1,0:T(8,128)(2,1)S(1)} %slice.12), channel_id=1, source_target_pairs={{0,28},{1,29},{2,30},{3,31}} | collective-permute-start | bytes 196616 | tf_op jit(solution)/shard_map/ppermute | solution.py:257
  93.8 7.1 %collective-permute-start.9 = (bf16[384,256]{1,0:T(8,128)(2,1)}, bf16[384,256]{1,0:T(8,128)(2,1)S(1)}, u32[]{:S(2)}, u32[]{:S(2)}) collective-permute-start(bf16[384,256]{1,0:T(8,128)(2,1)} %get-tuple-element.25.refs_1_), channel_id=1, source_target_pairs={{0,2},{1,3},{2,0},{3,1},{4,6},{5,7},{6,4},{7,5},{8,10},{9,11},{10,... | collective-permute-start | bytes 589832 | tf_op jit(solution)/shard_map/ppermute | solution.py:50
  95.3 9.6 %collective-permute-start.8 = (bf16[384,256]{1,0:T(8,128)(2,1)}, bf16[384,256]{1,0:T(8,128)(2,1)S(1)}, u32[]{:S(2)}, u32[]{:S(2)}) collective-permute-start(bf16[384,256]{1,0:T(8,128)(2,1)} %get-tuple-element.25.refs_1_), channel_id=1, source_target_pairs={{0,1},{1,0},{2,3},{3,2},{4,5},{5,4},{6,7},{7,6},{8,9},{9,8},{10,11... | collective-permute-start | bytes 589832 | tf_op jit(solution)/shard_map/ppermute | solution.py:50
  95.3 23.6 %collective-permute-start.18 = (bf16[384,256]{1,0:T(8,128)(2,1)}, bf16[384,256]{1,0:T(8,128)(2,1)S(1)}, u32[]{:S(2)}, u32[]{:S(2)}) collective-permute-start(bf16[384,256]{1,0:T(8,128)(2,1)} %get-tuple-element.33.refs_1_), channel_id=1, source_target_pairs={{0,2},{1,3},{2,0},{3,1},{4,6},{5,7},{6,4},{7,5},{8,10},{9,11},{10,... | collective-permute-start | bytes 589832 | tf_op jit(solution)/shard_map/ppermute | solution.py:50
  100.9 4.1 %collective-permute-start.10 = (bf16[384,256]{1,0:T(8,128)(2,1)S(1)}, bf16[384,256]{1,0:T(8,128)(2,1)S(1)}, u32[]{:S(2)}, u32[]{:S(2)}) collective-permute-start(bf16[384,256]{1,0:T(8,128)(2,1)S(1)} %collective-permute-done.9.refs_3_), channel_id=1, source_target_pairs={{0,1},{1,0},{2,3},{3,2},{4,5},{5,4},{6,7},{7,6},{8,9},{9,8},{10,11... | collective-permute-start | bytes 589832 | tf_op jit(solution)/shard_map/ppermute | solution.py:50
  118.5 15.8 %collective-permute-start.15 = (bf16[384,512]{1,0:T(8,128)(2,1)}, bf16[384,512]{1,0:T(8,128)(2,1)S(1)}, u32[]{:S(2)}, u32[]{:S(2)}) collective-permute-start(bf16[384,512]{1,0:T(8,128)(2,1)} %get-tuple-element.32), channel_id=1, source_target_pairs={{0,1},{1,0},{2,3},{3,2},{4,5},{5,4},{6,7},{7,6},{8,9},{9,8},{10,11... | collective-permute-start | bytes 1179656 | tf_op jit(solution)/shard_map/ppermute | solution.py:50
  118.9 1.8 %collective-permute-start.17 = (bf16[384,256]{1,0:T(8,128)(2,1)S(1)}, bf16[384,256]{1,0:T(8,128)(2,1)S(1)}, u32[]{:S(2)}, u32[]{:S(2)}) collective-permute-start(bf16[384,256]{1,0:T(8,128)(2,1)S(1)} %copy-done.8), channel_id=1, source_target_pairs={{0,1},{1,0},{2,3},{3,2},{4,5},{5,4},{6,7},{7,6},{8,9},{9,8},{10,11... | collective-permute-start | bytes 589832 | tf_op jit(solution)/shard_map/ppermute | solution.py:50
  119.0 2.0 %collective-permute-start.19 = (bf16[384,256]{1,0:T(8,128)(2,1)S(1)}, bf16[384,256]{1,0:T(8,128)(2,1)S(1)}, u32[]{:S(2)}, u32[]{:S(2)}) collective-permute-start(bf16[384,256]{1,0:T(8,128)(2,1)S(1)} %collective-permute-done.18.refs_3_), channel_id=1, source_target_pairs={{0,1},{1,0},{2,3},{3,2},{4,5},{5,4},{6,7},{7,6},{8,9},{9,8},{10,11... | collective-permute-start | bytes 589832 | tf_op jit(solution)/shard_map/ppermute | solution.py:50
  133.7 3.2 %collective-permute-start.21 = (bf16[384,512]{1,0:T(8,128)(2,1)}, bf16[384,512]{1,0:T(8,128)(2,1)S(1)}, u32[]{:S(2)}, u32[]{:S(2)}) collective-permute-start(bf16[384,512]{1,0:T(8,128)(2,1)} %get-tuple-element.38), channel_id=1, source_target_pairs={{0,1},{1,0},{2,3},{3,2},{4,5},{5,4},{6,7},{7,6},{8,9},{9,8},{10,11... | collective-permute-start | bytes 1179656 | tf_op jit(solution)/shard_map/ppermute | solution.py:50
  134.2 5.2 %collective-permute-start.14 = (bf16[384,512]{1,0:T(8,128)(2,1)S(1)}, bf16[384,512]{1,0:T(8,128)(2,1)S(1)}, u32[]{:S(2)}, u32[]{:S(2)}) collective-permute-start(bf16[384,512]{1,0:T(8,128)(2,1)S(1)} %copy-done.20), channel_id=1, source_target_pairs={{0,1},{1,0},{2,3},{3,2},{4,5},{5,4},{6,7},{7,6},{8,9},{9,8},{10,11... | collective-permute-start | bytes 1179656 | tf_op jit(solution)/shard_map/ppermute | solution.py:50
  134.4 12.4 %collective-permute-start.16 = (bf16[384,512]{1,0:T(8,128)(2,1)S(1)}, bf16[384,512]{1,0:T(8,128)(2,1)S(1)}, u32[]{:S(2)}, u32[]{:S(2)}) collective-permute-start(bf16[384,512]{1,0:T(8,128)(2,1)S(1)} %add_convert_fusion.3), channel_id=1, source_target_pairs={{0,2},{1,3},{2,0},{3,1},{4,6},{5,7},{6,4},{7,5},{8,10},{9,11},{10,... | collective-permute-start | bytes 1179656 | tf_op jit(solution)/shard_map/ppermute | solution.py:50
  136.8 10.2 %collective-permute-start.20 = (bf16[384,512]{1,0:T(8,128)(2,1)}, bf16[384,512]{1,0:T(8,128)(2,1)S(1)}, u32[]{:S(2)}, u32[]{:S(2)}) collective-permute-start(bf16[384,512]{1,0:T(8,128)(2,1)} %get-tuple-element.36), channel_id=1, source_target_pairs={{0,1},{1,0},{2,3},{3,2},{4,5},{5,4},{6,7},{7,6},{8,9},{9,8},{10,11... | collective-permute-start | bytes 1179656 | tf_op jit(solution)/shard_map/ppermute | solution.py:50
  138.1 16.8 %collective-permute-start.22 = (bf16[384,512]{1,0:T(8,128)(2,1)S(1)}, bf16[384,512]{1,0:T(8,128)(2,1)S(1)}, u32[]{:S(2)}, u32[]{:S(2)}) collective-permute-start(bf16[384,512]{1,0:T(8,128)(2,1)S(1)} %add_convert_fusion.1), channel_id=1, source_target_pairs={{0,2},{1,3},{2,0},{3,1},{4,6},{5,7},{6,4},{7,5},{8,10},{9,11},{10,... | collective-permute-start | bytes 1179656 | tf_op jit(solution)/shard_map/ppermute | solution.py:50
  (20 other events, 117.5 us)

commit v2 on v1

--- a/solution.py
+++ b/solution.py
@@ -6,6 +6,7 @@
 from jax.experimental import pallas as pl
 from jax.experimental.pallas import tpu as pltpu
 from jax.sharding import PartitionSpec as P
+
 
 norm_floor = 0.1
 head_floor = 0.05
@@ -15,7 +16,7 @@
 bf16 = jnp.bfloat16
 vmem = pl.BlockSpec(memory_space=pltpu.VMEM)
 smem = pl.BlockSpec(memory_space=pltpu.SMEM)
-roomy = pltpu.CompilerParams(vmem_limit_bytes=56 * 1024 * 1024)
+mebi = 1024 * 1024
 
 
 def mm(a, b):
@@ -50,35 +51,46 @@
     return lax.ppermute(x, axis, [(i, i ^ bit) for i in range(peers)])
 
 
-def gather_pieces(x, axis):
+def gather_pieces(x, axis, far=None):
     bit = lax.axis_size(axis) // 2
     pieces = {0: x}
+    if far is not None:
+        pieces[bit] = far
+        bit //= 2
     while bit:
         pieces.update({r | bit: swap(piece, axis, bit) for r, piece in pieces.items()})
         bit //= 2
     return [pieces[r] for r in range(len(pieces))]
 
 
-def scatter_pieces(pieces, axis):
-    peers = lax.axis_size(axis)
+def scatter_step(pieces, axis, bit):
+    keep = [r for r in pieces if not r & bit]
+    moved = {r: swap(pieces[r | bit].astype(bf16), axis, bit).astype(f32) for r in keep}
+    return {r: pieces[r].astype(f32) + moved[r] for r in keep}
+
+
+def scatter_near(pieces, axis):
     bit = 1
-    while bit < peers:
-        keep = [r for r in pieces if not r & bit]
-        moved = {r: swap(pieces[r | bit].astype(bf16), axis, bit).astype(f32) for r in keep}
-        pieces = {r: pieces[r].astype(f32) + moved[r] for r in keep}
+    while bit < lax.axis_size(axis) // 2:
+        pieces = scatter_step(pieces, axis, bit)
         bit *= 2
-    return pieces[0]
+    return {r: piece.astype(bf16) if r & bit else piece for r, piece in pieces.items()}
+
+
+def scatter_far(pieces, axis):
+    return scatter_step(pieces, axis, lax.axis_size(axis) // 2)[0]
 
 
 def unit(rows):
     return rows * lax.rsqrt(jnp.sum(rows * rows, axis=1, keepdims=True) + 1.0)
 
 
-def front_kernel(*refs, peers, heads, span):
+def front_kernel(*refs, peers, heads, span, part, first):
     me_ref = refs[0]
     piece_refs = refs[1 : 1 + peers]
-    gain_ref, weight_ref, cumul_ref, rate_ref = refs[1 + peers : 5 + peers]
-    whole_ref, local_ref, entry_ref, map_ref, proj_ref = refs[5 + peers :]
+    gain_ref, weight_ref, log_ref, rate_ref = refs[1 + peers : 5 + peers]
+    carry_refs = () if first else refs[5 + peers : 6 + peers]
+    whole_ref, local_ref, entry_ref, map_ref, proj_ref = refs[5 + peers + len(carry_refs) :]
     me = me_ref[0]
     length, slice_width = piece_refs[0].shape
     width = map_ref.shape[1]
@@ -101,11 +113,23 @@
     col_ids = lax.broadcasted_iota(jnp.int32, (span, span), 1)
     eye = (row_ids == col_ids).astype(f32)
     units = [(h, c) for h in range(heads) for c in range(pieces)]
+    begin = part * length
+    cumul_rows = jnp.dot(
+        jnp.concatenate(
+            [log_ref[h : h + 1, begin + c * span : begin + (c + 1) * span] for h, c in units]
+        ),
+        (row_ids <= col_ids).astype(f32),
+        precision=lax.Precision.HIGHEST,
+        preferred_element_type=f32,
+    )
 
     def operands(h, c):
         at = (slice(c * span, (c + 1) * span), slice(h * width, (h + 1) * width))
-        cumul_row = jnp.broadcast_to(cumul_ref[h, c : c + 1, :], (span, span))
-        rate = jnp.broadcast_to(rate_ref[h, c : c + 1, :], (span, span)).T
+        u = h * pieces + c
+        cumul_row = jnp.broadcast_to(cumul_rows[u : u + 1, :], (span, span))
+        rate = jnp.broadcast_to(
+            rate_ref[h : h + 1, begin + c * span : begin + (c + 1) * span], (span, span)
+        ).T
         cumul = cumul_row.T
         decay = jnp.where(
             row_ids >= col_ids, jnp.exp(jnp.minimum(cumul - cumul_row, 0.0)), 0.0
@@ -132,16 +156,13 @@
             inverses[u] = inverses[u] - mm_split(split, halves(inner))
         level += 1
     for h in range(heads):
-        carried = jnp.concatenate(
-            [
-                (
-                    lax.broadcasted_iota(jnp.int32, (width, width), 0)
-                    == lax.broadcasted_iota(jnp.int32, (width, width), 1)
-                ).astype(f32),
-                jnp.zeros((width, width), f32),
-            ],
-            axis=1,
-        )
+        if first:
+            carried = (
+                lax.broadcasted_iota(jnp.int32, (width, 2 * width), 0)
+                == lax.broadcasted_iota(jnp.int32, (width, 2 * width), 1)
+            ).astype(f32)
+        else:
+            carried = carry_refs[0][h]
         for c in range(pieces):
             at, cumul, cumul_row, rate, decay = operands(h, c)
             keys = proj_ref[(1,) + at]
@@ -165,7 +186,7 @@
             carried = jnp.concatenate(
                 [carried[:, :width], carried[:, width:] + tail[:, width:]], axis=1
             )
-        map_ref[h] = carried.astype(bf16)
+        map_ref[h] = carried.astype(map_ref.dtype)
 
 
 def joined(maps, h, width):
@@ -181,25 +202,27 @@
 
 
 def join_kernel(*refs):
-    out_ref = refs[-1]
+    out_ref, shift_ref = refs[-2:]
     width = out_ref.shape[1]
     for h in range(out_ref.shape[0]):
-        out_ref[h] = joined(refs[:-1], h, width).astype(bf16)
-
-
-def heads_kernel(*refs, count):
+        acc = joined(refs[:-2], h, width).astype(bf16)
+        out_ref[h] = acc
+        shift_ref[h] = acc[:, width:]
+
+
+def heads_kernel(*refs, count, parts):
     map_refs = refs[:count]
-    local_ref, entry_ref, gain_ref = refs[count : count + 3]
-    out_refs = refs[count + 3 :]
-    heads, length, width = local_ref.shape
-    rows = length // len(out_refs)
+    local_refs = refs[count : count + parts]
+    entry_refs = refs[count + parts : count + 2 * parts]
+    gain_ref = refs[count + 2 * parts]
+    out_refs = refs[count + 2 * parts + 1 :]
+    heads, _, width = local_refs[0].shape
     for h in range(heads):
         state = joined(map_refs, h, width)
         if state.shape[1] != width:
             state = state[:, width:]
         for part, out_ref in enumerate(out_refs):
-            at = slice(part * rows, (part + 1) * rows)
-            raw = local_ref[h, at, :] + mm(entry_ref[h, at, :], state)
+            raw = local_refs[part][h] + mm(entry_refs[part][h], state)
             out_ref[:, h * width : (h + 1) * width] = (
                 raw
                 * lax.rsqrt(jnp.mean(raw * raw, axis=1, keepdims=True) + head_floor)
@@ -241,14 +264,15 @@
     own_ref[...] = residual_ref[:, pl.ds(at, slice_width)]
 
 
-def call(kernel, outs, args, scratch=(), first_smem=True):
+def call(kernel, outs, args, scratch=(), first_smem=True, flops=10**9, room=8):
     return pl.pallas_call(
         kernel,
         out_shape=[jax.ShapeDtypeStruct(s, d) for s, d in outs],
         in_specs=[smem if first_smem and i == 0 else vmem for i in range(len(args))],
         out_specs=[vmem] * len(outs),
         scratch_shapes=list(scratch),
-        compiler_params=roomy,
+        compiler_params=pltpu.CompilerParams(vmem_limit_bytes=room * mebi),
+        cost_estimate=pl.CostEstimate(flops=flops, bytes_accessed=0, transcendentals=0),
     )(*args)
 
 
@@ -261,13 +285,21 @@
     peers = lax.axis_size(axis)
     width = maps.shape[1]
     window = 1
+    shift = None
     while window * radix < peers - 1:
         terms = [maps] + [shifted(maps, axis, window * k) for k in range(1, radix)]
-        maps = call(join_kernel, [(maps.shape, bf16)], terms, first_smem=False)[0]
+        maps, shift = call(
+            join_kernel,
+            [(maps.shape, bf16), (maps.shape[:2] + (width,), bf16)],
+            terms,
+            first_smem=False,
+        )
         window *= radix
+    if shift is None:
+        shift = maps[:, :, width:]
     offsets = list(range(1, peers, window))
     moved = [shifted(maps, axis, by) for by in offsets[:-1]]
-    return moved + [shifted(maps[:, :, width:], axis, by) for by in offsets[-1:]]
+    return moved + [shifted(shift, axis, by) for by in offsets[-1:]]
 
 
 def body(
@@ -289,57 +321,92 @@
     model = attn_gain.shape[0]
     peers = lax.axis_size("tp")
     me = lax.axis_index("tp").astype(jnp.int32).reshape(1)
-    span = min(128, length)
-    count = length // span
-    pieces = gather_pieces(layer_in, "tp")
-    cumul = jnp.cumsum(log_decay.reshape(local_heads, count, span), axis=2)
-    held = lax.optimization_barrier((out_weight, pieces[peers // 2]))
-    weight_pieces = gather_pieces(held[0], "tp")
-    whole, local, entry, maps = call(
-        functools.partial(front_kernel, peers=peers, heads=local_heads, span=span),
-        [
-            ((length, model), bf16),
-            ((local_heads, length, width), f32),
-            ((local_heads, length, width), bf16),
-            ((local_heads, width, 2 * width), bf16),
-        ],
-        [
-            me,
-            *pieces,
-            attn_gain.reshape(1, model),
-            qkv_weight,
-            cumul,
-            write_rate.reshape(local_heads, count, span),
-        ],
-        scratch=[pltpu.VMEM((3, length, local_heads * width), f32)],
-    )
+    parts = parts_of_block
+    rows = length // parts
+    span = min(128, rows)
+    pieces = [
+        gather_pieces(lax.slice_in_dim(layer_in, part * rows, (part + 1) * rows), "tp")
+        for part in range(parts)
+    ]
+    held = lax.optimization_barrier((out_weight, pieces[-1][peers // 2]))[0]
+    weight_far = swap(held, "tp", peers // 2)
+    wholes, locals_, entries = [], [], []
+    carried = ()
+    for part in range(parts):
+        last = part == parts - 1
+        whole, local, entry, maps = call(
+            functools.partial(
+                front_kernel,
+                peers=peers,
+                heads=local_heads,
+                span=span,
+                part=part,
+                first=part == 0,
+            ),
+            [
+                ((rows, model), bf16),
+                ((local_heads, rows, width), f32),
+                ((local_heads, rows, width), bf16),
+                ((local_heads, width, 2 * width), bf16 if last else f32),
+            ],
+            [
+                me,
+                *pieces[part],
+                attn_gain.reshape(1, model),
+                qkv_weight,
+                log_decay,
+                write_rate,
+                *carried,
+            ],
+            scratch=[pltpu.VMEM((3, rows, local_heads * width), f32)],
+            flops=8 * 10**9,
+            room=20,
+        )
+        carried = (maps,)
+        wholes.append(whole)
+        locals_.append(local)
+        entries.append(entry)
     before = earlier_maps(maps, "seq")
-    rows = length // parts_of_block
     heads_out = call(
-        functools.partial(heads_kernel, count=len(before)),
-        [((rows, local_heads * width), bf16)] * parts_of_block,
-        [*before, local, entry, head_gain.reshape(1, width)],
+        functools.partial(heads_kernel, count=len(before), parts=parts),
+        [((rows, local_heads * width), bf16)] * parts,
+        [*before, *locals_, *entries, head_gain.reshape(1, width)],
         first_smem=False,
-    )
+        flops=3 * 10**9,
+    )
+    weight_far, out_held, *heads_out = lax.optimization_barrier(
+        (weight_far, out_weight, *heads_out)
+    )
+    weight_pieces = gather_pieces(out_held, "tp", weight_far)
     results = []
-    gathered = [gather_pieces(part, "tp") for part in heads_out]
-    for part in range(parts_of_block):
-        own, *terms = call(
+    gathered = []
+    for shard in heads_out:
+        lead = swap
+        gathered.append(gather_pieces(shard, "tp", lead(shard, "tp", peers // 2)))
+    for part in range(parts):
+        back = call
+        far = scatter_far
+        own, *terms = back(
             functools.partial(back_kernel, peers=peers),
             [((rows, slice_width), f32)] + [((rows, slice_width), bf16)] * peers,
             [
                 me,
                 *gathered[part],
                 *weight_pieces,
-                lax.slice_in_dim(whole, part * rows, (part + 1) * rows),
+                wholes[part],
                 ffn_gain.reshape(1, model),
                 gate_weight,
                 up_weight,
                 down_weight,
             ],
             scratch=[pltpu.VMEM((rows, model), f32)],
-        )
-        shared = scatter_pieces(dict(enumerate(terms)), "tp")
+            flops=6 * 10**9,
+            room=28,
+        )
+        terms = scatter_near(dict(enumerate(terms)), "tp")
+        if part + 1 < parts:
+            gathered[part + 1], terms = lax.optimization_barrier((gathered[part + 1], terms))
+        shared = far(terms, "tp")
         results.append((own + shared).astype(bf16))
     return jnp.concatenate(results, axis=0)
 

time: 158 us -> 116 us (0.73)
  Pallas kernels: 44.8 us -> 27 us
  waiting for transfers between devices: 67.3 us -> 55.2 us
  local copies, waits for them, and re-layouts: 10.4 us -> 3.19 us
  starting transfers between devices: 29.6 us -> 26.3 us
  other arithmetic: 3.79 us -> 1.66 us
    pallas_call x5 -> x6, Pallas kernels: 44.8 us -> 27 us  [call(): pl.pallas_call(kernel, out_shape=[jax.ShapeDtypeStruct(s, d) for s, d in...]
    ppermute x18 -> x21, waiting for transfers between devices: 62.1 us -> 50.4 us  [swap(): return lax.ppermute(x, axis, [(i, i ^ bit) for i in range(peers)])]
    slice x2 -> x1, local copies, waits for them, and re-layouts: 4.89 us -> 1.25 us  [body(): lax.slice_in_dim(layer_in, part * rows, (part + 1) * rows)]
    ppermute x18 -> x21, starting transfers between devices: 12.6 us -> 9.11 us  [swap(): return lax.ppermute(x, axis, [(i, i ^ bit) for i in range(peers)])]
    reshape x2 -> x0, local copies, waits for them, and re-layouts: 1.99 us -> none  [the longest x1 1.29 us: body(): write_rate.reshape(local_heads, count, span)]
    unnamed x42 -> x22, local copies, waits for them, and re-layouts: 3.48 us -> 1.93 us
  transfers between devices with their start and end apart: 23 -> 26, of which waited for: 10 -> 11; matrix products, arithmetic and copies ran while one was open for 6% -> 0% of each run, Pallas kernels for 29% -> 13%
where the time goes in v2:
time: 116 us; the launch traced here: 114 us
  waiting for transfers between devices  55.2 us (48%)
  Pallas kernels  27 us (23%)
  starting transfers between devices  26.3 us (23%)
  local copies, waits for them, and re-layouts  3.19 us (3%)
  other arithmetic  1.66 us (1%)
    ppermute x21, waiting for transfers between devices, swap(): return lax.ppermute(x, axis, [(i, i ^ bit) for i in range(peers)])  50.4 us
    pallas_call x6, Pallas kernels, call(): pl.pallas_call(kernel, out_shape=[jax.ShapeDtypeStruct(s, d) for s, d in...  27 us
    ppermute x5, starting transfers between devices, shifted(): return lax.ppermute(x, axis, [(i, i + by) for i in range(peers - by)])  17.2 us
    ppermute x21, starting transfers between devices, swap(): return lax.ppermute(x, axis, [(i, i ^ bit) for i in range(peers)])  9.11 us
    ppermute x5, waiting for transfers between devices, shifted(): return lax.ppermute(x, axis, [(i, i + by) for i in range(peers - by)])  4.82 us
  transfers between devices with their start and end apart: 26, of which 11 were waited for; matrix products, arithmetic and copies ran while one was open for 0% of the time, Pallas kernels for 13%

profile of v2, /device:TPU:0, one launch (start us, length us, event | category | flops | bytes accessed | tf_op | source)
XLA Modules:
  0.0 113.7 jit_solution(5911274066284755013)
XLA Ops:
  0.0 1.3 %fusion = (bf16[384,512]{1,0:T(8,128)(2,1)S(1)}, bf16[384,512]{1,0:T(8,128)(2,1)S(1)}) fusion(bf16[768,512]{1,0:T(8,128)(2,1)} %param.11), kind=kLoop, calls=%fused_computation.6 | loop fusion | bytes 1572864 | tf_op jit(solution)/shard_map/slice | solution.py:328
  1.3 3.1 %collective-permute-start.5 = (bf16[384,512]{1,0:T(8,128)(2,1)S(1)}, bf16[384,512]{1,0:T(8,128)(2,1)S(1)}, u32[]{:S(2)}, u32[]{:S(2)}) collective-permute-start(bf16[384,512]{1,0:T(8,128)(2,1)S(1)} %get-tuple-element.71.refs_1_), channel_id=1, source_target_pairs={{0,2},{1,3},{2,0},{3,1},{4,6},{5,7},{6,4},{7,5},{8,10},{9,11},{10,... | collective-permute-start | bytes 1179656 | tf_op jit(solution)/shard_map/ppermute | solution.py:51
  4.4 9.9 %collective-permute-done.5.refs_3_ = bf16[384,512]{1,0:T(8,128)(2,1)S(1)} collective-permute-done((bf16[384,512]{1,0:T(8,128)(2,1)S(1)}, bf16[384,512]{1,0:T(8,128)(2,1)S(1)}, u32[]{:S(2)}, u32[]{:S(2)}) %collective-permute-start.5) | collective-permute-done | bytes 393248 | tf_op jit(solution)/shard_map/ppermute | solution.py:51
  14.8 7.1 %collective-permute-done.refs_3_ = bf16[384,512]{1,0:T(8,128)(2,1)S(1)} collective-permute-done((bf16[384,512]{1,0:T(8,128)(2,1)S(1)}, bf16[384,512]{1,0:T(8,128)(2,1)S(1)}, u32[]{:S(2)}, u32[]{:S(2)}) %collective-permute-start) | collective-permute-done | bytes 393248 | tf_op jit(solution)/shard_map/ppermute | solution.py:51
  21.9 1.7 %collective-permute-start.1 = (bf16[256,2048]{1,0:T(8,128)(2,1)S(1)}, bf16[256,2048]{1,0:T(8,128)(2,1)S(1)}, u32[]{:S(2)}, u32[]{:S(2)}) collective-permute-start(bf16[256,2048]{1,0:T(8,128)(2,1)S(1)} %copy-done.5), channel_id=1, source_target_pairs={{0,2},{1,3},{2,0},{3,1},{4,6},{5,7},{6,4},{7,5},{8,10},{9,11},{10,... | collective-permute-start | bytes 3145736 | tf_op jit(solution)/shard_map/ppermute | solution.py:51
  23.7 1.9 %copy-done = bf16[3,2048,256]{2,1,0:T(8,128)(2,1)S(1)} copy-done((bf16[3,2048,256]{2,1,0:T(8,128)(2,1)S(1)}, bf16[3,2048,256]{2,1,0:T(8,128)(2,1)}, u32[]{:S(2)}) %copy-start) | copy-done | bytes 3145752
  25.6 7.4 %shard_map.109 = (bf16[384,2048]{1,0:T(8,128)(2,1)S(1)}, f32[2,384,128]{2,1,0:T(8,128)S(1)}, bf16[2,384,128]{2,1,0:T(8,128)(2,1)S(1)}, f32[2,128,256]{2,1,0:T(8,128)S(1)}) custom-call(s32[1]{0:T(128)} %bitcast.refs_0_, bf16[384,512]{1,0:T(8,128)(2,1)S(1)} %get-tuple-element.71.refs_1_, bf16[384,512]{1,0:T(8,128)(2,1)S(1)} %collective-permute-done.4.refs_2_, ...), custom_call_target="tpu_custom_call" | custom-call | flops 8000000000 | tf_op jit(solution)/shard_map/pallas_call | solution.py:268
  33.0 6.3 %shard_map.110 = (bf16[384,2048]{1,0:T(8,128)(2,1)S(1)}, f32[2,384,128]{2,1,0:T(8,128)S(1)}, bf16[2,384,128]{2,1,0:T(8,128)(2,1)S(1)}, bf16[2,128,256]{2,1,0:T(8,128)(2,1)S(1)}) custom-call(s32[1]{0:T(128)} %bitcast.refs_0_, bf16[384,512]{1,0:T(8,128)(2,1)S(1)} %get-tuple-element.72.refs_1_, bf16[384,512]{1,0:T(8,128)(2,1)S(1)} %collective-permute-done.2.refs_2_, ...), custom_call_target="tpu_custom_call" | custom-call | flops 8000000000 | tf_op jit(solution)/shard_map/pallas_call | solution.py:268
  39.4 3.4 %collective-permute-start.7 = (bf16[2,128,256]{2,1,0:T(8,128)(2,1)S(1)}, bf16[2,128,256]{2,1,0:T(8,128)(2,1)S(1)}, u32[]{:S(2)}, u32[]{:S(2)}) collective-permute-start(bf16[2,128,256]{2,1,0:T(8,128)(2,1)S(1)} %get-tuple-element.40.refs_0_), channel_id=1, source_target_pairs={{0,4},{4,8},{8,12},{12,16},{16,20},{20,24},{24,28},{1,5},{5,9},{9,... | collective-permute-start | bytes 393224 | tf_op jit(solution)/shard_map/ppermute | solution.py:281
  42.8 3.5 %collective-permute-start.8 = (bf16[2,128,256]{2,1,0:T(8,128)(2,1)S(1)}, bf16[2,128,256]{2,1,0:T(8,128)(2,1)S(1)}, u32[]{:S(2)}, u32[]{:S(2)}) collective-permute-start(bf16[2,128,256]{2,1,0:T(8,128)(2,1)S(1)} %get-tuple-element.40.refs_0_), channel_id=1, source_target_pairs={{0,8},{4,12},{8,16},{12,20},{16,24},{20,28},{1,9},{5,13},{9,17},{1... | collective-permute-start | bytes 393224 | tf_op jit(solution)/shard_map/ppermute | solution.py:281
  46.3 3.1 %collective-permute-done.8.refs_2_ = bf16[2,128,256]{2,1,0:T(8,128)(2,1)S(1)} collective-permute-done((bf16[2,128,256]{2,1,0:T(8,128)(2,1)S(1)}, bf16[2,128,256]{2,1,0:T(8,128)(2,1)S(1)}, u32[]{:S(2)}, u32[]{:S(2)}) %collective-permute-start.8) | collective-permute-done | bytes 131104 | tf_op jit(solution)/shard_map/ppermute | solution.py:281
  49.8 5.4 %collective-permute-start.10 = (bf16[2,128,256]{2,1,0:T(8,128)(2,1)S(1)}, bf16[2,128,256]{2,1,0:T(8,128)(2,1)S(1)}, u32[]{:S(2)}, u32[]{:S(2)}) collective-permute-start(bf16[2,128,256]{2,1,0:T(8,128)(2,1)S(1)} %get-tuple-element.41), channel_id=1, source_target_pairs={{0,16},{4,20},{8,24},{12,28},{1,17},{5,21},{9,25},{13,29},{2,18},{... | collective-permute-start | bytes 393224 | tf_op jit(solution)/shard_map/ppermute | solution.py:281
  55.2 3.5 %collective-permute-start.9 = (bf16[2,128,256]{2,1,0:T(8,128)(2,1)S(1)}, bf16[2,128,256]{2,1,0:T(8,128)(2,1)S(1)}, u32[]{:S(2)}, u32[]{:S(2)}) collective-permute-start(bf16[2,128,256]{2,1,0:T(8,128)(2,1)S(1)} %get-tuple-element.41), channel_id=1, source_target_pairs={{0,4},{4,8},{8,12},{12,16},{16,20},{20,24},{24,28},{1,5},{5,9},{9,... | collective-permute-start | bytes 393224 | tf_op jit(solution)/shard_map/ppermute | solution.py:281
  58.6 1.5 %collective-permute-start.11 = (bf16[2,128,128]{2,1,0:T(8,128)(2,1)S(1)}, bf16[2,128,128]{2,1,0:T(8,128)(2,1)S(1)}, u32[]{:S(2)}, u32[]{:S(2)}) collective-permute-start(bf16[2,128,128]{2,1,0:T(8,128)(2,1)S(1)} %get-tuple-element.42), channel_id=1, source_target_pairs={{0,28},{1,29},{2,30},{3,31}} | collective-permute-start | bytes 196616 | tf_op jit(solution)/shard_map/ppermute | solution.py:281
  60.1 1.7 %collective-permute-done.11.refs_2_ = bf16[2,128,128]{2,1,0:T(8,128)(2,1)S(1)} collective-permute-done((bf16[2,128,128]{2,1,0:T(8,128)(2,1)S(1)}, bf16[2,128,128]{2,1,0:T(8,128)(2,1)S(1)}, u32[]{:S(2)}, u32[]{:S(2)}) %collective-permute-start.11) | collective-permute-done | bytes 65568 | tf_op jit(solution)/shard_map/ppermute | solution.py:281
  63.9 6.4 %collective-permute-done.13.refs_3_ = bf16[384,256]{1,0:T(8,128)(2,1)S(1)} collective-permute-done((bf16[384,256]{1,0:T(8,128)(2,1)S(1)}, bf16[384,256]{1,0:T(8,128)(2,1)S(1)}, u32[]{:S(2)}, u32[]{:S(2)}) %collective-permute-start.13) | collective-permute-done | bytes 196640 | tf_op jit(solution)/shard_map/ppermute | solution.py:51
  70.3 1.4 %collective-permute-done.14.refs_4_ = bf16[384,256]{1,0:T(8,128)(2,1)S(1)} collective-permute-done((bf16[384,256]{1,0:T(8,128)(2,1)S(1)}, bf16[384,256]{1,0:T(8,128)(2,1)S(1)}, u32[]{:S(2)}, u32[]{:S(2)}) %collective-permute-start.14) | collective-permute-done | bytes 196640 | tf_op jit(solution)/shard_map/ppermute | solution.py:51
  71.8 6.0 %shard_map.113 = (f32[384,512]{1,0:T(8,128)S(1)}, bf16[384,512]{1,0:T(8,128)(2,1)S(1)}, bf16[384,512]{1,0:T(8,128)(2,1)S(1)}, bf16[384,512]{1,0:T(8,128)(2,1)S(1)}, bf16[384,512]{1,0:T(8,128)(2,1)S(1)}) custom-call(s32[1]{0:T(128)} %bitcast.refs_0_, bf16[384,256]{1,0:T(8,128)(2,1)S(1)} %get-tuple-element.49.refs_1_, ...), custom_call_target="tpu_custom_call" | custom-call | flops 6000000000 | tf_op jit(solution)/shard_map/pallas_call | solution.py:268
  79.0 6.2 %collective-permute-done.18.refs_3_ = bf16[384,256]{1,0:T(8,128)(2,1)S(1)} collective-permute-done((bf16[384,256]{1,0:T(8,128)(2,1)S(1)}, bf16[384,256]{1,0:T(8,128)(2,1)S(1)}, u32[]{:S(2)}, u32[]{:S(2)}) %collective-permute-start.18) | collective-permute-done | bytes 196640 | tf_op jit(solution)/shard_map/ppermute | solution.py:51
  85.4 1.2 %collective-permute-done.19.refs_4_ = bf16[384,256]{1,0:T(8,128)(2,1)S(1)} collective-permute-done((bf16[384,256]{1,0:T(8,128)(2,1)S(1)}, bf16[384,256]{1,0:T(8,128)(2,1)S(1)}, u32[]{:S(2)}, u32[]{:S(2)}) %collective-permute-start.19) | collective-permute-done | bytes 196640 | tf_op jit(solution)/shard_map/ppermute | solution.py:51
  86.6 6.0 %shard_map.114 = (f32[384,512]{1,0:T(8,128)S(1)}, bf16[384,512]{1,0:T(8,128)(2,1)S(1)}, bf16[384,512]{1,0:T(8,128)(2,1)S(1)}, bf16[384,512]{1,0:T(8,128)(2,1)S(1)}, bf16[384,512]{1,0:T(8,128)(2,1)S(1)}) custom-call(s32[1]{0:T(128)} %bitcast.refs_0_, bf16[384,256]{1,0:T(8,128)(2,1)S(1)} %get-tuple-element.61.refs_1_, ...), custom_call_target="tpu_custom_call" | custom-call | flops 6000000000 | tf_op jit(solution)/shard_map/pallas_call | solution.py:268
  93.4 1.0 collective-permute-done.24
  95.1 9.7 %collective-permute-done.22 = bf16[384,512]{1,0:T(8,128)(2,1)S(1)} collective-permute-done((bf16[384,512]{1,0:T(8,128)(2,1)S(1)}, bf16[384,512]{1,0:T(8,128)(2,1)S(1)}, u32[]{:S(2)}, u32[]{:S(2)}) %collective-permute-start.22) | collective-permute-done | bytes 393248 | tf_op jit(solution)/shard_map/ppermute | solution.py:51
  105.0 7.6 %collective-permute-done.25 = bf16[384,512]{1,0:T(8,128)(2,1)S(1)} collective-permute-done((bf16[384,512]{1,0:T(8,128)(2,1)S(1)}, bf16[384,512]{1,0:T(8,128)(2,1)S(1)}, u32[]{:S(2)}, u32[]{:S(2)}) %collective-permute-start.25) | collective-permute-done | bytes 393248 | tf_op jit(solution)/shard_map/ppermute | solution.py:51
  (63 shorter events, 7.4 us)
Async XLA Ops:
  1.3 13.0 %collective-permute-start.5 = (bf16[384,512]{1,0:T(8,128)(2,1)S(1)}, bf16[384,512]{1,0:T(8,128)(2,1)S(1)}, u32[]{:S(2)}, u32[]{:S(2)}) collective-permute-start(bf16[384,512]{1,0:T(8,128)(2,1)S(1)} %get-tuple-element.71.refs_1_), channel_id=1, source_target_pairs={{0,2},{1,3},{2,0},{3,1},{4,6},{5,7},{6,4},{7,5},{8,10},{9,11},{10,... | collective-permute-start | bytes 1179656 | tf_op jit(solution)/shard_map/ppermute | solution.py:51
  4.3 17.5 %collective-permute-start = (bf16[384,512]{1,0:T(8,128)(2,1)S(1)}, bf16[384,512]{1,0:T(8,128)(2,1)S(1)}, u32[]{:S(2)}, u32[]{:S(2)}) collective-permute-start(bf16[384,512]{1,0:T(8,128)(2,1)S(1)} %get-tuple-element.72.refs_1_), channel_id=1, source_target_pairs={{0,2},{1,3},{2,0},{3,1},{4,6},{5,7},{6,4},{7,5},{8,10},{9,11},{10,... | collective-permute-start | bytes 1179656 | tf_op jit(solution)/shard_map/ppermute | solution.py:51
  4.4 19.2 %collective-permute-start.4 = (bf16[384,512]{1,0:T(8,128)(2,1)S(1)}, bf16[384,512]{1,0:T(8,128)(2,1)S(1)}, u32[]{:S(2)}, u32[]{:S(2)}) collective-permute-start(bf16[384,512]{1,0:T(8,128)(2,1)S(1)} %get-tuple-element.71.refs_1_), channel_id=1, source_target_pairs={{0,1},{1,0},{2,3},{3,2},{4,5},{5,4},{6,7},{7,6},{8,9},{9,8},{10,11... | collective-permute-start | bytes 1179656 | tf_op jit(solution)/shard_map/ppermute | solution.py:51
  14.3 9.3 %collective-permute-start.6 = (bf16[384,512]{1,0:T(8,128)(2,1)S(1)}, bf16[384,512]{1,0:T(8,128)(2,1)}, u32[]{:S(2)}, u32[]{:S(2)}) collective-permute-start(bf16[384,512]{1,0:T(8,128)(2,1)S(1)} %collective-permute-done.5.refs_3_), channel_id=1, source_target_pairs={{0,1},{1,0},{2,3},{3,2},{4,5},{5,4},{6,7},{7,6},{8,9},{9,8},{10,11... | collective-permute-start | bytes 1179656 | tf_op jit(solution)/shard_map/ppermute | solution.py:51
  14.3 18.7 %collective-permute-start.2 = (bf16[384,512]{1,0:T(8,128)(2,1)S(1)}, bf16[384,512]{1,0:T(8,128)(2,1)S(1)}, u32[]{:S(2)}, u32[]{:S(2)}) collective-permute-start(bf16[384,512]{1,0:T(8,128)(2,1)S(1)} %get-tuple-element.72.refs_1_), channel_id=1, source_target_pairs={{0,1},{1,0},{2,3},{3,2},{4,5},{5,4},{6,7},{7,6},{8,9},{9,8},{10,11... | collective-permute-start | bytes 1179656 | tf_op jit(solution)/shard_map/ppermute | solution.py:51
  21.9 41.0 %collective-permute-start.1 = (bf16[256,2048]{1,0:T(8,128)(2,1)S(1)}, bf16[256,2048]{1,0:T(8,128)(2,1)S(1)}, u32[]{:S(2)}, u32[]{:S(2)}) collective-permute-start(bf16[256,2048]{1,0:T(8,128)(2,1)S(1)} %copy-done.5), channel_id=1, source_target_pairs={{0,2},{1,3},{2,0},{3,1},{4,6},{5,7},{6,4},{7,5},{8,10},{9,11},{10,... | collective-permute-start | bytes 3145736 | tf_op jit(solution)/shard_map/ppermute | solution.py:51
  23.6 9.4 %collective-permute-start.3 = (bf16[384,512]{1,0:T(8,128)(2,1)S(1)}, bf16[384,512]{1,0:T(8,128)(2,1)S(1)}, u32[]{:S(2)}, u32[]{:S(2)}) collective-permute-start(bf16[384,512]{1,0:T(8,128)(2,1)S(1)} %collective-permute-done.refs_3_), channel_id=1, source_target_pairs={{0,1},{1,0},{2,3},{3,2},{4,5},{5,4},{6,7},{7,6},{8,9},{9,8},{10,11... | collective-permute-start | bytes 1179656 | tf_op jit(solution)/shard_map/ppermute | solution.py:51
  39.4 6.9 %collective-permute-start.7 = (bf16[2,128,256]{2,1,0:T(8,128)(2,1)S(1)}, bf16[2,128,256]{2,1,0:T(8,128)(2,1)S(1)}, u32[]{:S(2)}, u32[]{:S(2)}) collective-permute-start(bf16[2,128,256]{2,1,0:T(8,128)(2,1)S(1)} %get-tuple-element.40.refs_0_), channel_id=1, source_target_pairs={{0,4},{4,8},{8,12},{12,16},{16,20},{20,24},{24,28},{1,5},{5,9},{9,... | collective-permute-start | bytes 393224 | tf_op jit(solution)/shard_map/ppermute | solution.py:281
  42.8 6.6 %collective-permute-start.8 = (bf16[2,128,256]{2,1,0:T(8,128)(2,1)S(1)}, bf16[2,128,256]{2,1,0:T(8,128)(2,1)S(1)}, u32[]{:S(2)}, u32[]{:S(2)}) collective-permute-start(bf16[2,128,256]{2,1,0:T(8,128)(2,1)S(1)} %get-tuple-element.40.refs_0_), channel_id=1, source_target_pairs={{0,8},{4,12},{8,16},{12,20},{16,24},{20,28},{1,9},{5,13},{9,17},{1... | collective-permute-start | bytes 393224 | tf_op jit(solution)/shard_map/ppermute | solution.py:281
  49.8 12.1 %collective-permute-start.10 = (bf16[2,128,256]{2,1,0:T(8,128)(2,1)S(1)}, bf16[2,128,256]{2,1,0:T(8,128)(2,1)S(1)}, u32[]{:S(2)}, u32[]{:S(2)}) collective-permute-start(bf16[2,128,256]{2,1,0:T(8,128)(2,1)S(1)} %get-tuple-element.41), channel_id=1, source_target_pairs={{0,16},{4,20},{8,24},{12,28},{1,17},{5,21},{9,25},{13,29},{2,18},{... | collective-permute-start | bytes 393224 | tf_op jit(solution)/shard_map/ppermute | solution.py:281
  55.2 6.7 %collective-permute-start.9 = (bf16[2,128,256]{2,1,0:T(8,128)(2,1)S(1)}, bf16[2,128,256]{2,1,0:T(8,128)(2,1)S(1)}, u32[]{:S(2)}, u32[]{:S(2)}) collective-permute-start(bf16[2,128,256]{2,1,0:T(8,128)(2,1)S(1)} %get-tuple-element.41), channel_id=1, source_target_pairs={{0,4},{4,8},{8,12},{12,16},{16,20},{20,24},{24,28},{1,5},{5,9},{9,... | collective-permute-start | bytes 393224 | tf_op jit(solution)/shard_map/ppermute | solution.py:281
  58.6 3.2 %collective-permute-start.11 = (bf16[2,128,128]{2,1,0:T(8,128)(2,1)S(1)}, bf16[2,128,128]{2,1,0:T(8,128)(2,1)S(1)}, u32[]{:S(2)}, u32[]{:S(2)}) collective-permute-start(bf16[2,128,128]{2,1,0:T(8,128)(2,1)S(1)} %get-tuple-element.42), channel_id=1, source_target_pairs={{0,28},{1,29},{2,30},{3,31}} | collective-permute-start | bytes 196616 | tf_op jit(solution)/shard_map/ppermute | solution.py:281
  62.8 8.9 %collective-permute-start.15 = (bf16[256,2048]{1,0:T(8,128)(2,1)S(1)}, bf16[256,2048]{1,0:T(8,128)(2,1)S(1)}, u32[]{:S(2)}, u32[]{:S(2)}) collective-permute-start(bf16[256,2048]{1,0:T(8,128)(2,1)S(1)} %copy-done.5), channel_id=1, source_target_pairs={{0,1},{1,0},{2,3},{3,2},{4,5},{5,4},{6,7},{7,6},{8,9},{9,8},{10,11... | collective-permute-start | bytes 3145736 | tf_op jit(solution)/shard_map/ppermute | solution.py:51
  62.9 8.8 %collective-permute-start.16 = (bf16[256,2048]{1,0:T(8,128)(2,1)S(1)}, bf16[256,2048]{1,0:T(8,128)(2,1)S(1)}, u32[]{:S(2)}, u32[]{:S(2)}) collective-permute-start(bf16[256,2048]{1,0:T(8,128)(2,1)S(1)} %collective-permute-done.1.refs_7_), channel_id=1, source_target_pairs={{0,1},{1,0},{2,3},{3,2},{4,5},{5,4},{6,7},{7,6},{8,9},{9,8},{10,11... | collective-permute-start | bytes 3145736 | tf_op jit(solution)/shard_map/ppermute | solution.py:51
  63.4 6.9 %collective-permute-start.13 = (bf16[384,256]{1,0:T(8,128)(2,1)S(1)}, bf16[384,256]{1,0:T(8,128)(2,1)S(1)}, u32[]{:S(2)}, u32[]{:S(2)}) collective-permute-start(bf16[384,256]{1,0:T(8,128)(2,1)S(1)} %get-tuple-element.49.refs_1_), channel_id=1, source_target_pairs={{0,2},{1,3},{2,0},{3,1},{4,6},{5,7},{6,4},{7,5},{8,10},{9,11},{10,... | collective-permute-start | bytes 589832 | tf_op jit(solution)/shard_map/ppermute | solution.py:51
  63.9 6.4 %collective-permute-start.12 = (bf16[384,256]{1,0:T(8,128)(2,1)S(1)}, bf16[384,256]{1,0:T(8,128)(2,1)S(1)}, u32[]{:S(2)}, u32[]{:S(2)}) collective-permute-start(bf16[384,256]{1,0:T(8,128)(2,1)S(1)} %get-tuple-element.49.refs_1_), channel_id=1, source_target_pairs={{0,1},{1,0},{2,3},{3,2},{4,5},{5,4},{6,7},{7,6},{8,9},{9,8},{10,11... | collective-permute-start | bytes 589832 | tf_op jit(solution)/shard_map/ppermute | solution.py:51
  77.8 7.4 %collective-permute-start.20 = (bf16[384,512]{1,0:T(8,128)(2,1)S(1)}, bf16[384,512]{1,0:T(8,128)(2,1)S(1)}, u32[]{:S(2)}, u32[]{:S(2)}) collective-permute-start(bf16[384,512]{1,0:T(8,128)(2,1)S(1)} %get-tuple-element.56), channel_id=1, source_target_pairs={{0,1},{1,0},{2,3},{3,2},{4,5},{5,4},{6,7},{7,6},{8,9},{9,8},{10,11... | collective-permute-start | bytes 1179656 | tf_op jit(solution)/shard_map/ppermute | solution.py:51
  78.0 7.2 %collective-permute-start.18 = (bf16[384,256]{1,0:T(8,128)(2,1)S(1)}, bf16[384,256]{1,0:T(8,128)(2,1)S(1)}, u32[]{:S(2)}, u32[]{:S(2)}) collective-permute-start(bf16[384,256]{1,0:T(8,128)(2,1)S(1)} %get-tuple-element.61.refs_1_), channel_id=1, source_target_pairs={{0,2},{1,3},{2,0},{3,1},{4,6},{5,7},{6,4},{7,5},{8,10},{9,11},{10,... | collective-permute-start | bytes 589832 | tf_op jit(solution)/shard_map/ppermute | solution.py:51
  78.5 6.8 %collective-permute-start.21 = (bf16[384,512]{1,0:T(8,128)(2,1)S(1)}, bf16[384,512]{1,0:T(8,128)(2,1)S(1)}, u32[]{:S(2)}, u32[]{:S(2)}) collective-permute-start(bf16[384,512]{1,0:T(8,128)(2,1)S(1)} %get-tuple-element.58), channel_id=1, source_target_pairs={{0,1},{1,0},{2,3},{3,2},{4,5},{5,4},{6,7},{7,6},{8,9},{9,8},{10,11... | collective-permute-start | bytes 1179656 | tf_op jit(solution)/shard_map/ppermute | solution.py:51
  78.6 6.8 %collective-permute-start.17 = (bf16[384,256]{1,0:T(8,128)(2,1)S(1)}, bf16[384,256]{1,0:T(8,128)(2,1)S(1)}, u32[]{:S(2)}, u32[]{:S(2)}) collective-permute-start(bf16[384,256]{1,0:T(8,128)(2,1)S(1)} %get-tuple-element.61.refs_1_), channel_id=1, source_target_pairs={{0,1},{1,0},{2,3},{3,2},{4,5},{5,4},{6,7},{7,6},{8,9},{9,8},{10,11... | collective-permute-start | bytes 589832 | tf_op jit(solution)/shard_map/ppermute | solution.py:51
  92.6 1.8 %collective-permute-start.24 = (bf16[384,512]{1,0:T(8,128)(2,1)S(1)}, bf16[384,512]{1,0:T(8,128)(2,1)S(1)}, u32[]{:S(2)}, u32[]{:S(2)}) collective-permute-start(bf16[384,512]{1,0:T(8,128)(2,1)S(1)} %get-tuple-element.70), channel_id=1, source_target_pairs={{0,1},{1,0},{2,3},{3,2},{4,5},{5,4},{6,7},{7,6},{8,9},{9,8},{10,11... | collective-permute-start | bytes 1179656 | tf_op jit(solution)/shard_map/ppermute | solution.py:51
  92.8 12.0 %collective-permute-start.22 = (bf16[384,512]{1,0:T(8,128)(2,1)S(1)}, bf16[384,512]{1,0:T(8,128)(2,1)S(1)}, u32[]{:S(2)}, u32[]{:S(2)}) collective-permute-start(bf16[384,512]{1,0:T(8,128)(2,1)S(1)} %add_convert_fusion.3), channel_id=1, source_target_pairs={{0,2},{1,3},{2,0},{3,1},{4,6},{5,7},{6,4},{7,5},{8,10},{9,11},{10,... | collective-permute-start | bytes 1179656 | tf_op jit(solution)/shard_map/ppermute | solution.py:51
  93.3 11.7 %collective-permute-start.23 = (bf16[384,512]{1,0:T(8,128)(2,1)S(1)}, bf16[384,512]{1,0:T(8,128)(2,1)S(1)}, u32[]{:S(2)}, u32[]{:S(2)}) collective-permute-start(bf16[384,512]{1,0:T(8,128)(2,1)S(1)} %get-tuple-element.68), channel_id=1, source_target_pairs={{0,1},{1,0},{2,3},{3,2},{4,5},{5,4},{6,7},{7,6},{8,9},{9,8},{10,11... | collective-permute-start | bytes 1179656 | tf_op jit(solution)/shard_map/ppermute | solution.py:51
  94.5 18.1 %collective-permute-start.25 = (bf16[384,512]{1,0:T(8,128)(2,1)S(1)}, bf16[384,512]{1,0:T(8,128)(2,1)S(1)}, u32[]{:S(2)}, u32[]{:S(2)}) collective-permute-start(bf16[384,512]{1,0:T(8,128)(2,1)S(1)} %add_convert_fusion.1), channel_id=1, source_target_pairs={{0,2},{1,3},{2,0},{3,1},{4,6},{5,7},{6,4},{7,5},{8,10},{9,11},{10,... | collective-permute-start | bytes 1179656 | tf_op jit(solution)/shard_map/ppermute | solution.py:51
  (13 other events, 167.2 us)

commit v3 on v2

--- a/solution.py
+++ b/solution.py
@@ -10,7 +10,7 @@
 
 norm_floor = 0.1
 head_floor = 0.05
-parts_of_block = 2
+parts_of_block = 3
 radix = 3
 f32 = jnp.float32
 bf16 = jnp.bfloat16
@@ -324,17 +324,19 @@
     parts = parts_of_block
     rows = length // parts
     span = min(128, rows)
-    pieces = [
-        gather_pieces(lax.slice_in_dim(layer_in, part * rows, (part + 1) * rows), "tp")
-        for part in range(parts)
-    ]
+    pieces = []
+    for part in range(parts):
+        cross = swap
+        shard = lax.slice_in_dim(layer_in, part * rows, (part + 1) * rows)
+        pieces.append(gather_pieces(shard, "tp", cross(shard, "tp", peers // 2)))
     held = lax.optimization_barrier((out_weight, pieces[-1][peers // 2]))[0]
     weight_far = swap(held, "tp", peers // 2)
     wholes, locals_, entries = [], [], []
     carried = ()
     for part in range(parts):
         last = part == parts - 1
-        whole, local, entry, maps = call(
+        front = call
+        whole, local, entry, maps = front(
             functools.partial(
                 front_kernel,
                 peers=peers,

time: 116 us -> 116 us (level)
  waiting for transfers between devices: 55.2 us -> 42.6 us
  starting transfers between devices: 26.3 us -> 37.3 us
  Pallas kernels: 27 us -> 29.2 us
    ppermute x21 -> x30, waiting for transfers between devices: 50.4 us -> 38.2 us  [swap(): return lax.ppermute(x, axis, [(i, i ^ bit) for i in range(peers)])]
    ppermute x21 -> x30, starting transfers between devices: 9.11 us -> 19.6 us  [swap(): return lax.ppermute(x, axis, [(i, i ^ bit) for i in range(peers)])]
    pallas_call x6 -> x8, Pallas kernels: 27 us -> 29.2 us  [call(): pl.pallas_call(kernel, out_shape=[jax.ShapeDtypeStruct(s, d) for s, d in...]
  transfers between devices with their start and end apart: 26 -> 35, of which waited for: 11 -> 13; matrix products, arithmetic and copies ran while one was open for 0% -> 1% of each run, Pallas kernels for 13% -> 18%
where the time goes in v3:
time: 116 us; the launch traced here: 114 us
  waiting for transfers between devices  42.6 us (37%)
  starting transfers between devices  37.3 us (32%)
  Pallas kernels  29.2 us (25%)
  local copies, waits for them, and re-layouts  3.18 us (3%)
  other arithmetic  1.68 us (1%)
    ppermute x30, waiting for transfers between devices, swap(): return lax.ppermute(x, axis, [(i, i ^ bit) for i in range(peers)])  38.2 us
    pallas_call x8, Pallas kernels, call(): pl.pallas_call(kernel, out_shape=[jax.ShapeDtypeStruct(s, d) for s, d in...  29.2 us
    ppermute x30, starting transfers between devices, swap(): return lax.ppermute(x, axis, [(i, i ^ bit) for i in range(peers)])  19.6 us
    ppermute x5, starting transfers between devices, shifted(): return lax.ppermute(x, axis, [(i, i + by) for i in range(peers - by)])  17.7 us
    ppermute x5, waiting for transfers between devices, shifted(): return lax.ppermute(x, axis, [(i, i + by) for i in range(peers - by)])  4.34 us
  transfers between devices with their start and end apart: 35, of which 13 were waited for; matrix products, arithmetic and copies ran while one was open for 1% of the time, Pallas kernels for 18%

profile of v3, /device:TPU:0, one launch (start us, length us, event | category | flops | bytes accessed | tf_op | source)
XLA Modules:
  0.0 114.3 jit_solution(12775142095123961673)
XLA Ops:
  1.3 3.1 %collective-permute-start.8 = (bf16[256,512]{1,0:T(8,128)(2,1)S(1)}, bf16[256,512]{1,0:T(8,128)(2,1)S(1)}, u32[]{:S(2)}, u32[]{:S(2)}) collective-permute-start(bf16[256,512]{1,0:T(8,128)(2,1)S(1)} %get-tuple-element.105.refs_1_), channel_id=1, source_target_pairs={{0,2},{1,3},{2,0},{3,1},{4,6},{5,7},{6,4},{7,5},{8,10},{9,11},{10,... | collective-permute-start | bytes 786440 | tf_op jit(solution)/shard_map/ppermute | solution.py:51
  4.4 1.9 %collective-permute-start.5 = (bf16[256,512]{1,0:T(8,128)(2,1)S(1)}, bf16[256,512]{1,0:T(8,128)(2,1)S(1)}, u32[]{:S(2)}, u32[]{:S(2)}) collective-permute-start(bf16[256,512]{1,0:T(8,128)(2,1)S(1)} %get-tuple-element.107.refs_1_), channel_id=1, source_target_pairs={{0,2},{1,3},{2,0},{3,1},{4,6},{5,7},{6,4},{7,5},{8,10},{9,11},{10,... | collective-permute-start | bytes 786440 | tf_op jit(solution)/shard_map/ppermute | solution.py:51
  6.4 5.1 %collective-permute-done.8.refs_3_ = bf16[256,512]{1,0:T(8,128)(2,1)S(1)} collective-permute-done((bf16[256,512]{1,0:T(8,128)(2,1)S(1)}, bf16[256,512]{1,0:T(8,128)(2,1)S(1)}, u32[]{:S(2)}, u32[]{:S(2)}) %collective-permute-start.8) | collective-permute-done | bytes 262176 | tf_op jit(solution)/shard_map/ppermute | solution.py:51
  12.0 5.1 %collective-permute-done.refs_3_ = bf16[256,512]{1,0:T(8,128)(2,1)S(1)} collective-permute-done((bf16[256,512]{1,0:T(8,128)(2,1)S(1)}, bf16[256,512]{1,0:T(8,128)(2,1)S(1)}, u32[]{:S(2)}, u32[]{:S(2)}) %collective-permute-start) | collective-permute-done | bytes 262176 | tf_op jit(solution)/shard_map/ppermute | solution.py:51
  17.1 2.1 %collective-permute-start.1 = (bf16[256,2048]{1,0:T(8,128)(2,1)S(1)}, bf16[256,2048]{1,0:T(8,128)(2,1)S(1)}, u32[]{:S(2)}, u32[]{:S(2)}) collective-permute-start(bf16[256,2048]{1,0:T(8,128)(2,1)S(1)} %copy-done.5), channel_id=1, source_target_pairs={{0,2},{1,3},{2,0},{3,1},{4,6},{5,7},{6,4},{7,5},{8,10},{9,11},{10,... | collective-permute-start | bytes 3145736 | tf_op jit(solution)/shard_map/ppermute | solution.py:51
  19.2 3.5 %collective-permute-done.5.refs_3_ = bf16[256,512]{1,0:T(8,128)(2,1)S(1)} collective-permute-done((bf16[256,512]{1,0:T(8,128)(2,1)S(1)}, bf16[256,512]{1,0:T(8,128)(2,1)S(1)}, u32[]{:S(2)}, u32[]{:S(2)}) %collective-permute-start.5) | collective-permute-done | bytes 262176 | tf_op jit(solution)/shard_map/ppermute | solution.py:51
  23.3 1.9 %copy-done = bf16[3,2048,256]{2,1,0:T(8,128)(2,1)S(1)} copy-done((bf16[3,2048,256]{2,1,0:T(8,128)(2,1)S(1)}, bf16[3,2048,256]{2,1,0:T(8,128)(2,1)}, u32[]{:S(2)}) %copy-start) | copy-done | bytes 3145752
  25.1 5.2 %shard_map.109 = (bf16[256,2048]{1,0:T(8,128)(2,1)S(1)}, f32[2,256,128]{2,1,0:T(8,128)S(1)}, bf16[2,256,128]{2,1,0:T(8,128)(2,1)S(1)}, f32[2,128,256]{2,1,0:T(8,128)S(1)}) custom-call(s32[1]{0:T(128)} %bitcast.refs_0_, bf16[256,512]{1,0:T(8,128)(2,1)S(1)} %get-tuple-element.105.refs_1_, bf16[256,512]{1,0:T(8,128)(2,1)S(1)} %collective-permute-done.7.refs_2_, ...), custom_call_target="tpu_custom_call" | custom-call | flops 8000000000 | tf_op jit(solution)/shard_map/pallas_call | solution.py:268
  30.3 5.2 %shard_map.110 = (bf16[256,2048]{1,0:T(8,128)(2,1)S(1)}, f32[2,256,128]{2,1,0:T(8,128)S(1)}, bf16[2,256,128]{2,1,0:T(8,128)(2,1)S(1)}, f32[2,128,256]{2,1,0:T(8,128)S(1)}) custom-call(s32[1]{0:T(128)} %bitcast.refs_0_, bf16[256,512]{1,0:T(8,128)(2,1)S(1)} %get-tuple-element.107.refs_1_, bf16[256,512]{1,0:T(8,128)(2,1)S(1)} %collective-permute-done.4.refs_2_, ...), custom_call_target="tpu_custom_call" | custom-call | flops 8000000000 | tf_op jit(solution)/shard_map/pallas_call | solution.py:268
  35.6 5.2 %shard_map.111 = (bf16[256,2048]{1,0:T(8,128)(2,1)S(1)}, f32[2,256,128]{2,1,0:T(8,128)S(1)}, bf16[2,256,128]{2,1,0:T(8,128)(2,1)S(1)}, bf16[2,128,256]{2,1,0:T(8,128)(2,1)S(1)}) custom-call(s32[1]{0:T(128)} %bitcast.refs_0_, bf16[256,512]{1,0:T(8,128)(2,1)S(1)} %get-tuple-element.106.refs_1_, bf16[256,512]{1,0:T(8,128)(2,1)S(1)} %collective-permute-done.2.refs_2_, ...), custom_call_target="tpu_custom_call" | custom-call | flops 8000000000 | tf_op jit(solution)/shard_map/pallas_call | solution.py:268
  40.8 3.9 %collective-permute-start.10 = (bf16[2,128,256]{2,1,0:T(8,128)(2,1)S(1)}, bf16[2,128,256]{2,1,0:T(8,128)(2,1)S(1)}, u32[]{:S(2)}, u32[]{:S(2)}) collective-permute-start(bf16[2,128,256]{2,1,0:T(8,128)(2,1)S(1)} %get-tuple-element.58.refs_0_), channel_id=1, source_target_pairs={{0,4},{4,8},{8,12},{12,16},{16,20},{20,24},{24,28},{1,5},{5,9},{9,... | collective-permute-start | bytes 393224 | tf_op jit(solution)/shard_map/ppermute | solution.py:281
  44.7 3.5 %collective-permute-start.11 = (bf16[2,128,256]{2,1,0:T(8,128)(2,1)S(1)}, bf16[2,128,256]{2,1,0:T(8,128)(2,1)S(1)}, u32[]{:S(2)}, u32[]{:S(2)}) collective-permute-start(bf16[2,128,256]{2,1,0:T(8,128)(2,1)S(1)} %get-tuple-element.58.refs_0_), channel_id=1, source_target_pairs={{0,8},{4,12},{8,16},{12,20},{16,24},{20,28},{1,9},{5,13},{9,17},{1... | collective-permute-start | bytes 393224 | tf_op jit(solution)/shard_map/ppermute | solution.py:281
  48.2 2.6 %collective-permute-done.11.refs_2_ = bf16[2,128,256]{2,1,0:T(8,128)(2,1)S(1)} collective-permute-done((bf16[2,128,256]{2,1,0:T(8,128)(2,1)S(1)}, bf16[2,128,256]{2,1,0:T(8,128)(2,1)S(1)}, u32[]{:S(2)}, u32[]{:S(2)}) %collective-permute-start.11) | collective-permute-done | bytes 131104 | tf_op jit(solution)/shard_map/ppermute | solution.py:281
  51.1 3.5 %collective-permute-start.12 = (bf16[2,128,256]{2,1,0:T(8,128)(2,1)S(1)}, bf16[2,128,256]{2,1,0:T(8,128)(2,1)S(1)}, u32[]{:S(2)}, u32[]{:S(2)}) collective-permute-start(bf16[2,128,256]{2,1,0:T(8,128)(2,1)S(1)} %get-tuple-element.59), channel_id=1, source_target_pairs={{0,4},{4,8},{8,12},{12,16},{16,20},{20,24},{24,28},{1,5},{5,9},{9,... | collective-permute-start | bytes 393224 | tf_op jit(solution)/shard_map/ppermute | solution.py:281
  54.6 5.4 %collective-permute-start.13 = (bf16[2,128,256]{2,1,0:T(8,128)(2,1)S(1)}, bf16[2,128,256]{2,1,0:T(8,128)(2,1)S(1)}, u32[]{:S(2)}, u32[]{:S(2)}) collective-permute-start(bf16[2,128,256]{2,1,0:T(8,128)(2,1)S(1)} %get-tuple-element.59), channel_id=1, source_target_pairs={{0,16},{4,20},{8,24},{12,28},{1,17},{5,21},{9,25},{13,29},{2,18},{... | collective-permute-start | bytes 393224 | tf_op jit(solution)/shard_map/ppermute | solution.py:281
  61.5 1.7 %collective-permute-done.14.refs_2_ = bf16[2,128,128]{2,1,0:T(8,128)(2,1)S(1)} collective-permute-done((bf16[2,128,128]{2,1,0:T(8,128)(2,1)S(1)}, bf16[2,128,128]{2,1,0:T(8,128)(2,1)S(1)}, u32[]{:S(2)}, u32[]{:S(2)}) %collective-permute-start.14) | collective-permute-done | bytes 65568 | tf_op jit(solution)/shard_map/ppermute | solution.py:281
  66.3 4.0 %collective-permute-done.16.refs_3_ = bf16[256,256]{1,0:T(8,128)(2,1)S(1)} collective-permute-done((bf16[256,256]{1,0:T(8,128)(2,1)S(1)}, bf16[256,256]{1,0:T(8,128)(2,1)S(1)}, u32[]{:S(2)}, u32[]{:S(2)}) %collective-permute-start.16) | collective-permute-done | bytes 131104 | tf_op jit(solution)/shard_map/ppermute | solution.py:51
  71.7 4.1 %shard_map.114 = (f32[256,512]{1,0:T(8,128)S(1)}, bf16[256,512]{1,0:T(8,128)(2,1)S(1)}, bf16[256,512]{1,0:T(8,128)(2,1)S(1)}, bf16[256,512]{1,0:T(8,128)(2,1)S(1)}, bf16[256,512]{1,0:T(8,128)(2,1)S(1)}) custom-call(s32[1]{0:T(128)} %bitcast.refs_0_, bf16[256,256]{1,0:T(8,128)(2,1)S(1)} %get-tuple-element.70.refs_1_, ...), custom_call_target="tpu_custom_call" | custom-call | flops 6000000000 | tf_op jit(solution)/shard_map/pallas_call | solution.py:268
  78.0 3.7 %collective-permute-done.21.refs_3_ = bf16[256,256]{1,0:T(8,128)(2,1)S(1)} collective-permute-done((bf16[256,256]{1,0:T(8,128)(2,1)S(1)}, bf16[256,256]{1,0:T(8,128)(2,1)S(1)}, u32[]{:S(2)}, u32[]{:S(2)}) %collective-permute-start.21) | collective-permute-done | bytes 131104 | tf_op jit(solution)/shard_map/ppermute | solution.py:51
  83.1 4.1 %shard_map.115 = (f32[256,512]{1,0:T(8,128)S(1)}, bf16[256,512]{1,0:T(8,128)(2,1)S(1)}, bf16[256,512]{1,0:T(8,128)(2,1)S(1)}, bf16[256,512]{1,0:T(8,128)(2,1)S(1)}, bf16[256,512]{1,0:T(8,128)(2,1)S(1)}) custom-call(s32[1]{0:T(128)} %bitcast.refs_0_, bf16[256,256]{1,0:T(8,128)(2,1)S(1)} %get-tuple-element.82.refs_1_, ...), custom_call_target="tpu_custom_call" | custom-call | flops 6000000000 | tf_op jit(solution)/shard_map/pallas_call | solution.py:268
  89.5 3.7 %collective-permute-done.27.refs_3_ = bf16[256,256]{1,0:T(8,128)(2,1)S(1)} collective-permute-done((bf16[256,256]{1,0:T(8,128)(2,1)S(1)}, bf16[256,256]{1,0:T(8,128)(2,1)S(1)}, u32[]{:S(2)}, u32[]{:S(2)}) %collective-permute-start.27) | collective-permute-done | bytes 131104 | tf_op jit(solution)/shard_map/ppermute | solution.py:51
  96.1 4.1 %shard_map.116 = (f32[256,512]{1,0:T(8,128)S(1)}, bf16[256,512]{1,0:T(8,128)(2,1)S(1)}, bf16[256,512]{1,0:T(8,128)(2,1)S(1)}, bf16[256,512]{1,0:T(8,128)(2,1)S(1)}, bf16[256,512]{1,0:T(8,128)(2,1)S(1)}) custom-call(s32[1]{0:T(128)} %bitcast.refs_0_, bf16[256,256]{1,0:T(8,128)(2,1)S(1)} %get-tuple-element.95.refs_1_, ...), custom_call_target="tpu_custom_call" | custom-call | flops 6000000000 | tf_op jit(solution)/shard_map/pallas_call | solution.py:268
  104.2 3.8 %collective-permute-done.31 = bf16[256,512]{1,0:T(8,128)(2,1)S(1)} collective-permute-done((bf16[256,512]{1,0:T(8,128)(2,1)S(1)}, bf16[256,512]{1,0:T(8,128)(2,1)S(1)}, u32[]{:S(2)}, u32[]{:S(2)}) %collective-permute-start.31) | collective-permute-done | bytes 262176 | tf_op jit(solution)/shard_map/ppermute | solution.py:51
  108.2 5.0 %collective-permute-done.34 = bf16[256,512]{1,0:T(8,128)(2,1)S(1)} collective-permute-done((bf16[256,512]{1,0:T(8,128)(2,1)S(1)}, bf16[256,512]{1,0:T(8,128)(2,1)S(1)}, u32[]{:S(2)}, u32[]{:S(2)}) %collective-permute-start.34) | collective-permute-done | bytes 262176 | tf_op jit(solution)/shard_map/ppermute | solution.py:51
  (86 shorter events, 22.4 us)
Async XLA Ops:
  1.3 10.2 %collective-permute-start.8 = (bf16[256,512]{1,0:T(8,128)(2,1)S(1)}, bf16[256,512]{1,0:T(8,128)(2,1)S(1)}, u32[]{:S(2)}, u32[]{:S(2)}) collective-permute-start(bf16[256,512]{1,0:T(8,128)(2,1)S(1)} %get-tuple-element.105.refs_1_), channel_id=1, source_target_pairs={{0,2},{1,3},{2,0},{3,1},{4,6},{5,7},{6,4},{7,5},{8,10},{9,11},{10,... | collective-permute-start | bytes 786440 | tf_op jit(solution)/shard_map/ppermute | solution.py:51
  4.3 12.8 %collective-permute-start = (bf16[256,512]{1,0:T(8,128)(2,1)S(1)}, bf16[256,512]{1,0:T(8,128)(2,1)S(1)}, u32[]{:S(2)}, u32[]{:S(2)}) collective-permute-start(bf16[256,512]{1,0:T(8,128)(2,1)S(1)} %get-tuple-element.106.refs_1_), channel_id=1, source_target_pairs={{0,2},{1,3},{2,0},{3,1},{4,6},{5,7},{6,4},{7,5},{8,10},{9,11},{10,... | collective-permute-start | bytes 786440 | tf_op jit(solution)/shard_map/ppermute | solution.py:51
  4.4 12.7 %collective-permute-start.7 = (bf16[256,512]{1,0:T(8,128)(2,1)S(1)}, bf16[256,512]{1,0:T(8,128)(2,1)S(1)}, u32[]{:S(2)}, u32[]{:S(2)}) collective-permute-start(bf16[256,512]{1,0:T(8,128)(2,1)S(1)} %get-tuple-element.105.refs_1_), channel_id=1, source_target_pairs={{0,1},{1,0},{2,3},{3,2},{4,5},{5,4},{6,7},{7,6},{8,9},{9,8},{10,11... | collective-permute-start | bytes 786440 | tf_op jit(solution)/shard_map/ppermute | solution.py:51
  4.4 18.3 %collective-permute-start.5 = (bf16[256,512]{1,0:T(8,128)(2,1)S(1)}, bf16[256,512]{1,0:T(8,128)(2,1)S(1)}, u32[]{:S(2)}, u32[]{:S(2)}) collective-permute-start(bf16[256,512]{1,0:T(8,128)(2,1)S(1)} %get-tuple-element.107.refs_1_), channel_id=1, source_target_pairs={{0,2},{1,3},{2,0},{3,1},{4,6},{5,7},{6,4},{7,5},{8,10},{9,11},{10,... | collective-permute-start | bytes 786440 | tf_op jit(solution)/shard_map/ppermute | solution.py:51
  11.5 11.2 %collective-permute-start.9 = (bf16[256,512]{1,0:T(8,128)(2,1)S(1)}, bf16[256,512]{1,0:T(8,128)(2,1)S(1)}, u32[]{:S(2)}, u32[]{:S(2)}) collective-permute-start(bf16[256,512]{1,0:T(8,128)(2,1)S(1)} %collective-permute-done.8.refs_3_), channel_id=1, source_target_pairs={{0,1},{1,0},{2,3},{3,2},{4,5},{5,4},{6,7},{7,6},{8,9},{9,8},{10,11... | collective-permute-start | bytes 786440 | tf_op jit(solution)/shard_map/ppermute | solution.py:51
  11.5 18.8 %collective-permute-start.4 = (bf16[256,512]{1,0:T(8,128)(2,1)S(1)}, bf16[256,512]{1,0:T(8,128)(2,1)S(1)}, u32[]{:S(2)}, u32[]{:S(2)}) collective-permute-start(bf16[256,512]{1,0:T(8,128)(2,1)S(1)} %get-tuple-element.107.refs_1_), channel_id=1, source_target_pairs={{0,1},{1,0},{2,3},{3,2},{4,5},{5,4},{6,7},{7,6},{8,9},{9,8},{10,11... | collective-permute-start | bytes 786440 | tf_op jit(solution)/shard_map/ppermute | solution.py:51
  17.1 18.4 %collective-permute-start.2 = (bf16[256,512]{1,0:T(8,128)(2,1)S(1)}, bf16[256,512]{1,0:T(8,128)(2,1)S(1)}, u32[]{:S(2)}, u32[]{:S(2)}) collective-permute-start(bf16[256,512]{1,0:T(8,128)(2,1)S(1)} %get-tuple-element.106.refs_1_), channel_id=1, source_target_pairs={{0,1},{1,0},{2,3},{3,2},{4,5},{5,4},{6,7},{7,6},{8,9},{9,8},{10,11... | collective-permute-start | bytes 786440 | tf_op jit(solution)/shard_map/ppermute | solution.py:51
  17.1 47.1 %collective-permute-start.1 = (bf16[256,2048]{1,0:T(8,128)(2,1)S(1)}, bf16[256,2048]{1,0:T(8,128)(2,1)S(1)}, u32[]{:S(2)}, u32[]{:S(2)}) collective-permute-start(bf16[256,2048]{1,0:T(8,128)(2,1)S(1)} %copy-done.5), channel_id=1, source_target_pairs={{0,2},{1,3},{2,0},{3,1},{4,6},{5,7},{6,4},{7,5},{8,10},{9,11},{10,... | collective-permute-start | bytes 3145736 | tf_op jit(solution)/shard_map/ppermute | solution.py:51
  22.7 12.8 %collective-permute-start.3 = (bf16[256,512]{1,0:T(8,128)(2,1)S(1)}, bf16[256,512]{1,0:T(8,128)(2,1)S(1)}, u32[]{:S(2)}, u32[]{:S(2)}) collective-permute-start(bf16[256,512]{1,0:T(8,128)(2,1)S(1)} %collective-permute-done.refs_3_), channel_id=1, source_target_pairs={{0,1},{1,0},{2,3},{3,2},{4,5},{5,4},{6,7},{7,6},{8,9},{9,8},{10,11... | collective-permute-start | bytes 786440 | tf_op jit(solution)/shard_map/ppermute | solution.py:51
  22.7 7.6 %collective-permute-start.6 = (bf16[256,512]{1,0:T(8,128)(2,1)S(1)}, bf16[256,512]{1,0:T(8,128)(2,1)S(1)}, u32[]{:S(2)}, u32[]{:S(2)}) collective-permute-start(bf16[256,512]{1,0:T(8,128)(2,1)S(1)} %collective-permute-done.5.refs_3_), channel_id=1, source_target_pairs={{0,1},{1,0},{2,3},{3,2},{4,5},{5,4},{6,7},{7,6},{8,9},{9,8},{10,11... | collective-permute-start | bytes 786440 | tf_op jit(solution)/shard_map/ppermute | solution.py:51
  40.8 7.4 %collective-permute-start.10 = (bf16[2,128,256]{2,1,0:T(8,128)(2,1)S(1)}, bf16[2,128,256]{2,1,0:T(8,128)(2,1)S(1)}, u32[]{:S(2)}, u32[]{:S(2)}) collective-permute-start(bf16[2,128,256]{2,1,0:T(8,128)(2,1)S(1)} %get-tuple-element.58.refs_0_), channel_id=1, source_target_pairs={{0,4},{4,8},{8,12},{12,16},{16,20},{20,24},{24,28},{1,5},{5,9},{9,... | collective-permute-start | bytes 393224 | tf_op jit(solution)/shard_map/ppermute | solution.py:281
  44.7 6.1 %collective-permute-start.11 = (bf16[2,128,256]{2,1,0:T(8,128)(2,1)S(1)}, bf16[2,128,256]{2,1,0:T(8,128)(2,1)S(1)}, u32[]{:S(2)}, u32[]{:S(2)}) collective-permute-start(bf16[2,128,256]{2,1,0:T(8,128)(2,1)S(1)} %get-tuple-element.58.refs_0_), channel_id=1, source_target_pairs={{0,8},{4,12},{8,16},{12,20},{16,24},{20,28},{1,9},{5,13},{9,17},{1... | collective-permute-start | bytes 393224 | tf_op jit(solution)/shard_map/ppermute | solution.py:281
  51.1 12.1 %collective-permute-start.12 = (bf16[2,128,256]{2,1,0:T(8,128)(2,1)S(1)}, bf16[2,128,256]{2,1,0:T(8,128)(2,1)S(1)}, u32[]{:S(2)}, u32[]{:S(2)}) collective-permute-start(bf16[2,128,256]{2,1,0:T(8,128)(2,1)S(1)} %get-tuple-element.59), channel_id=1, source_target_pairs={{0,4},{4,8},{8,12},{12,16},{16,20},{20,24},{24,28},{1,5},{5,9},{9,... | collective-permute-start | bytes 393224 | tf_op jit(solution)/shard_map/ppermute | solution.py:281
  54.6 8.6 %collective-permute-start.13 = (bf16[2,128,256]{2,1,0:T(8,128)(2,1)S(1)}, bf16[2,128,256]{2,1,0:T(8,128)(2,1)S(1)}, u32[]{:S(2)}, u32[]{:S(2)}) collective-permute-start(bf16[2,128,256]{2,1,0:T(8,128)(2,1)S(1)} %get-tuple-element.59), channel_id=1, source_target_pairs={{0,16},{4,20},{8,24},{12,28},{1,17},{5,21},{9,25},{13,29},{2,18},{... | collective-permute-start | bytes 393224 | tf_op jit(solution)/shard_map/ppermute | solution.py:281
  64.2 7.4 %collective-permute-start.18 = (bf16[256,2048]{1,0:T(8,128)(2,1)S(1)}, bf16[256,2048]{1,0:T(8,128)(2,1)S(1)}, u32[]{:S(2)}, u32[]{:S(2)}) collective-permute-start(bf16[256,2048]{1,0:T(8,128)(2,1)S(1)} %copy-done.5), channel_id=1, source_target_pairs={{0,1},{1,0},{2,3},{3,2},{4,5},{5,4},{6,7},{7,6},{8,9},{9,8},{10,11... | collective-permute-start | bytes 3145736 | tf_op jit(solution)/shard_map/ppermute | solution.py:51
  64.3 7.3 %collective-permute-start.19 = (bf16[256,2048]{1,0:T(8,128)(2,1)S(1)}, bf16[256,2048]{1,0:T(8,128)(2,1)S(1)}, u32[]{:S(2)}, u32[]{:S(2)}) collective-permute-start(bf16[256,2048]{1,0:T(8,128)(2,1)S(1)} %collective-permute-done.1.refs_7_), channel_id=1, source_target_pairs={{0,1},{1,0},{2,3},{3,2},{4,5},{5,4},{6,7},{7,6},{8,9},{9,8},{10,11... | collective-permute-start | bytes 3145736 | tf_op jit(solution)/shard_map/ppermute | solution.py:51
  75.8 6.0 %collective-permute-start.23 = (bf16[256,512]{1,0:T(8,128)(2,1)S(1)}, bf16[256,512]{1,0:T(8,128)(2,1)S(1)}, u32[]{:S(2)}, u32[]{:S(2)}) collective-permute-start(bf16[256,512]{1,0:T(8,128)(2,1)S(1)} %get-tuple-element.77), channel_id=1, source_target_pairs={{0,1},{1,0},{2,3},{3,2},{4,5},{5,4},{6,7},{7,6},{8,9},{9,8},{10,11... | collective-permute-start | bytes 786440 | tf_op jit(solution)/shard_map/ppermute | solution.py:51
  87.3 7.5 %collective-permute-start.29 = (bf16[256,512]{1,0:T(8,128)(2,1)S(1)}, bf16[256,512]{1,0:T(8,128)(2,1)S(1)}, u32[]{:S(2)}, u32[]{:S(2)}) collective-permute-start(bf16[256,512]{1,0:T(8,128)(2,1)S(1)} %get-tuple-element.90), channel_id=1, source_target_pairs={{0,1},{1,0},{2,3},{3,2},{4,5},{5,4},{6,7},{7,6},{8,9},{9,8},{10,11... | collective-permute-start | bytes 786440 | tf_op jit(solution)/shard_map/ppermute | solution.py:51
  89.0 5.9 %collective-permute-start.30 = (bf16[256,512]{1,0:T(8,128)(2,1)S(1)}, bf16[256,512]{1,0:T(8,128)(2,1)S(1)}, u32[]{:S(2)}, u32[]{:S(2)}) collective-permute-start(bf16[256,512]{1,0:T(8,128)(2,1)S(1)} %get-tuple-element.92), channel_id=1, source_target_pairs={{0,1},{1,0},{2,3},{3,2},{4,5},{5,4},{6,7},{7,6},{8,9},{9,8},{10,11... | collective-permute-start | bytes 786440 | tf_op jit(solution)/shard_map/ppermute | solution.py:51
  89.1 5.8 %collective-permute-start.26 = (bf16[256,256]{1,0:T(8,128)(2,1)S(1)}, bf16[256,256]{1,0:T(8,128)(2,1)S(1)}, u32[]{:S(2)}, u32[]{:S(2)}) collective-permute-start(bf16[256,256]{1,0:T(8,128)(2,1)S(1)} %get-tuple-element.95.refs_1_), channel_id=1, source_target_pairs={{0,1},{1,0},{2,3},{3,2},{4,5},{5,4},{6,7},{7,6},{8,9},{9,8},{10,11... | collective-permute-start | bytes 393224 | tf_op jit(solution)/shard_map/ppermute | solution.py:51
  93.3 9.2 %collective-permute-start.25 = (bf16[256,512]{1,0:T(8,128)(2,1)S(1)}, bf16[256,512]{1,0:T(8,128)(2,1)S(1)}, u32[]{:S(2)}, u32[]{:S(2)}) collective-permute-start(bf16[256,512]{1,0:T(8,128)(2,1)S(1)} %add_convert_fusion.5), channel_id=1, source_target_pairs={{0,2},{1,3},{2,0},{3,1},{4,6},{5,7},{6,4},{7,5},{8,10},{9,11},{10,... | collective-permute-start | bytes 786440 | tf_op jit(solution)/shard_map/ppermute | solution.py:51
  94.9 13.1 %collective-permute-start.31 = (bf16[256,512]{1,0:T(8,128)(2,1)S(1)}, bf16[256,512]{1,0:T(8,128)(2,1)S(1)}, u32[]{:S(2)}, u32[]{:S(2)}) collective-permute-start(bf16[256,512]{1,0:T(8,128)(2,1)S(1)} %add_convert_fusion.3), channel_id=1, source_target_pairs={{0,2},{1,3},{2,0},{3,1},{4,6},{5,7},{6,4},{7,5},{8,10},{9,11},{10,... | collective-permute-start | bytes 786440 | tf_op jit(solution)/shard_map/ppermute | solution.py:51
  100.3 7.9 %collective-permute-start.32 = (bf16[256,512]{1,0:T(8,128)(2,1)S(1)}, bf16[256,512]{1,0:T(8,128)(2,1)S(1)}, u32[]{:S(2)}, u32[]{:S(2)}) collective-permute-start(bf16[256,512]{1,0:T(8,128)(2,1)S(1)} %get-tuple-element.102), channel_id=1, source_target_pairs={{0,1},{1,0},{2,3},{3,2},{4,5},{5,4},{6,7},{7,6},{8,9},{9,8},{10,11... | collective-permute-start | bytes 786440 | tf_op jit(solution)/shard_map/ppermute | solution.py:51
  102.7 10.5 %collective-permute-start.34 = (bf16[256,512]{1,0:T(8,128)(2,1)S(1)}, bf16[256,512]{1,0:T(8,128)(2,1)S(1)}, u32[]{:S(2)}, u32[]{:S(2)}) collective-permute-start(bf16[256,512]{1,0:T(8,128)(2,1)S(1)} %add_convert_fusion.1), channel_id=1, source_target_pairs={{0,2},{1,3},{2,0},{3,1},{4,6},{5,7},{6,4},{7,5},{8,10},{9,11},{10,... | collective-permute-start | bytes 786440 | tf_op jit(solution)/shard_map/ppermute | solution.py:51
  (22 other events, 189.6 us)
